TPU v7x, 512 devices: a whole 4x8x8 slice. The times are simulated.
512 devices in a mesh: wall: 128 (over z, y, core), span: 4 (over x).
Axes of the slice: x: 4, y: 8, z: 8, core: 2. Of those that a mesh axis runs over, the one named last changes fastest.
Arguments:
- random_planes: float32 [8, 3, 2048, 4096], P(None, None, 'wall', 'span'), may hold values from -6 to 6
- previous: float32 [3, 2048, 4096], P(None, 'wall', 'span'), may hold values from -6 to 6
- half_width: int32 [2048], P('wall'), may hold values from 1 to 32
- time_scale: float32 [3, 2048], P(None, 'wall'), may hold values from 1 to 16
- lund_factor: float32 [6, 2048], P(None, 'wall'), may hold values from -4 to 4
- mean_velocity: float32 [2048], P('wall'), may hold values from 0.5 to 1.5
Outputs:
- velocity: float32 [8, 3, 2048, 4096], P(None, None, 'wall', 'span')
- filter_state: float32 [3, 2048, 4096], P(None, 'wall', 'span')
All inputs are finite; a program needn't handle non-finite values.
Results may differ from a plain program's by a relative error of at most 0.000064.
Values sent between devices are 32-bit elements; how exact they have to be, the bound alone decides.
No kernel may reach another device: no remote copies, remote signals or barrier semaphores. Data moves between devices by JAX's collectives and lax.ppermute only.
A program may use at most 128 MiB of HBM per device.

v0:
```python
import math

import jax
import jax.numpy as jnp
from jax import lax
from jax.sharding import PartitionSpec as P

HMAX = 32
HZ = 24


def shifted(shard, axis, by):
    length = lax.axis_size(axis)
    pairs = [(i, i + by) for i in range(length) if 0 <= i + by < length]
    return lax.ppermute(shard, axis, pairs)


def with_halo(block, sides, width):
    for axis, dim in sides:
        count = lax.axis_size(axis)
        forward = [(i, i + 1) for i in range(count - 1)]
        forward.append((count - 1, 0))
        backward = [(target, source) for source, target in forward]
        low = lax.ppermute(
            lax.slice_in_dim(block, block.shape[dim] - width, None, axis=dim), axis, forward
        )
        high = lax.ppermute(lax.slice_in_dim(block, 0, width, axis=dim), axis, backward)
        block = jnp.concatenate([low, block, high], axis=dim)
    return block


def band_matrix(widths, reach):
    height = widths.shape[0]
    row_index = lax.broadcasted_iota(jnp.int32, (height, height + 2 * reach), 0)
    column_index = lax.broadcasted_iota(jnp.int32, (height, height + 2 * reach), 1)
    offset = column_index - row_index - reach
    spread = widths.astype(jnp.float32)[:, None]
    distance = offset.astype(jnp.float32)
    shaped = jnp.where(
        jnp.abs(offset) <= widths[:, None],
        jnp.exp(-2.0 * math.pi * distance * distance / (spread * spread)),
        0.0,
    )
    return shaped / jnp.sqrt(jnp.sum(shaped * shaped, axis=1, keepdims=True))


def shards(random_planes, previous, half_width, time_scale, lund_factor, mean_velocity):
    highest = lax.Precision.HIGHEST
    row_count = random_planes.shape[2]
    depth = -(-HMAX // row_count)
    lower_parts = []
    upper_parts = []
    for distance in range(1, depth + 1):
        lower_parts.insert(0, shifted(random_planes, "wall", distance))
        upper_parts.append(shifted(random_planes, "wall", -distance))
    extended = jnp.concatenate(lower_parts + [random_planes] + upper_parts, axis=2)
    wall_band = band_matrix(half_width, HMAX)
    wall_pass = jnp.einsum("ik,sckz->sciz", wall_band, extended, precision=highest)
    margin = with_halo(wall_pass, (("span", 3),), HZ)
    layout = wall_pass.shape
    flat_margin = margin.reshape(-1, margin.shape[3])
    span_band = band_matrix(jnp.full((layout[3],), HZ, jnp.int32), HZ)
    filtered = jnp.einsum("rk,zk->rz", flat_margin, span_band, precision=highest).reshape(layout)
    retain = jnp.exp(-math.pi / (2.0 * time_scale))[:, :, None]
    inject = jnp.sqrt(1.0 - jnp.exp(-math.pi / time_scale))[:, :, None]
    factor = lund_factor[:, :, None]
    current = previous
    velocities = []
    for instant in range(filtered.shape[0]):
        current = retain * current + inject * filtered[instant]
        stream = mean_velocity[:, None] + factor[0] * current[0]
        normal = factor[1] * current[0] + factor[2] * current[1]
        spanwise = factor[3] * current[0] + factor[4] * current[1] + factor[5] * current[2]
        velocities.append(jnp.stack([stream, normal, spanwise]))
    return (jnp.stack(velocities), current)


def solution(mesh):
    in_specs = (
        P(None, None, "wall", "span"),
        P(None, "wall", "span"),
        P("wall"),
        P(None, "wall"),
        P(None, "wall"),
        P("wall"),
    )
    out_specs = (P(None, None, "wall", "span"), P(None, "wall", "span"))
    return jax.shard_map(shards, mesh=mesh, in_specs=in_specs, out_specs=out_specs, check_vma=False)
```

profile of v0, /device:TPU:254, one launch (start us, length us, event | category | flops | bytes accessed | tf_op | source)
XLA Modules:
  0.0 96.4 jit_solution(4101410824191879029)
XLA Ops:
  0.6 0.0 copy-start
  0.6 4.8 %collective-permute-start = (f32[8,3,16,1024]{3,2,1,0:T(8,128)}, f32[8,3,16,1024]{3,2,1,0:T(8,128)S(1)}, u32[]{:S(2)}, u32[]{:S(2)}) collective-permute-start(f32[8,3,16,1024]{3,2,1,0:T(8,128)} %param.6), channel_id=1, source_target_pairs={{0,8},{4,12},{8,16},{12,20},{16,24},{20,28},{24,32},{28,36},{32,40... | collective-permute-start | bytes 4718600 | tf_op jit(solution)/shard_map/ppermute | solution.py:15
  5.5 1.9 %collective-permute-start.1 = (f32[8,3,16,1024]{3,2,1,0:T(8,128)}, f32[8,3,16,1024]{3,2,1,0:T(8,128)S(1)}, u32[]{:S(2)}, u32[]{:S(2)}) collective-permute-start(f32[8,3,16,1024]{3,2,1,0:T(8,128)} %param.6), channel_id=1, source_target_pairs={{0,4},{4,8},{8,12},{12,16},{16,20},{20,24},{24,28},{28,32},{32,36}... | collective-permute-start | bytes 4718600 | tf_op jit(solution)/shard_map/ppermute | solution.py:15
  7.4 3.6 %collective-permute-start.2 = (f32[8,3,16,1024]{3,2,1,0:T(8,128)}, f32[8,3,16,1024]{3,2,1,0:T(8,128)S(1)}, u32[]{:S(2)}, u32[]{:S(2)}) collective-permute-start(f32[8,3,16,1024]{3,2,1,0:T(8,128)} %param.6), channel_id=1, source_target_pairs={{4,0},{8,4},{12,8},{16,12},{20,16},{24,20},{28,24},{32,28},{36,32}... | collective-permute-start | bytes 4718600 | tf_op jit(solution)/shard_map/ppermute | solution.py:15
  11.1 1.9 %collective-permute-start.3 = (f32[8,3,16,1024]{3,2,1,0:T(8,128)}, f32[8,3,16,1024]{3,2,1,0:T(8,128)S(1)}, u32[]{:S(2)}, u32[]{:S(2)}) collective-permute-start(f32[8,3,16,1024]{3,2,1,0:T(8,128)} %param.6), channel_id=1, source_target_pairs={{8,0},{12,4},{16,8},{20,12},{24,16},{28,20},{32,24},{36,28},{40,32... | collective-permute-start | bytes 4718600 | tf_op jit(solution)/shard_map/ppermute | solution.py:15
  13.0 0.7 convert_multiply_fusion
  13.6 0.8 multiply_reduce_fusion.1
  14.5 1.5 %slice_bitcast_fusion.5 = (f32[16]{0:T(128)S(1)}, f32[16]{0:T(128)S(1)}, f32[16]{0:T(128)S(1)}, f32[16]{0:T(128)S(1)}, f32[16]{0:T(128)}, /*index=5*/f32[16]{0:T(128)}) fusion(f32[6,16]{1,0:T(8,128)} %param.10), kind=kLoop, calls=%fused_computation.93 | loop fusion | bytes 768 | tf_op jit(solution)/shard_map/slice | solution.py:71
  16.0 1.2 %multiply_reduce_fusion = f32[1024]{0:T(1024)S(1)} fusion(), kind=kLoop, calls=%fused_computation.6 | loop fusion | flops 12073984 | bytes 4096 | tf_op jit(solution)/shard_map/reduce_sum | solution.py:44
  17.2 23.4 %collective-permute-done = f32[8,3,16,1024]{3,2,1,0:T(8,128)S(1)} collective-permute-done((f32[8,3,16,1024]{3,2,1,0:T(8,128)}, f32[8,3,16,1024]{3,2,1,0:T(8,128)S(1)}, u32[]{:S(2)}, u32[]{:S(2)}) %collective-permute-start) | collective-permute-done | bytes 1572896 | tf_op jit(solution)/shard_map/ppermute | solution.py:15
  40.5 0.1 constant_dynamic-update-slice_fusion.4
  40.7 15.2 %collective-permute-done.1 = f32[8,3,16,1024]{3,2,1,0:T(8,128)S(1)} collective-permute-done((f32[8,3,16,1024]{3,2,1,0:T(8,128)}, f32[8,3,16,1024]{3,2,1,0:T(8,128)S(1)}, u32[]{:S(2)}, u32[]{:S(2)}) %collective-permute-start.1) | collective-permute-done | bytes 1572896 | tf_op jit(solution)/shard_map/ppermute | solution.py:15
  55.9 0.1 constant_dynamic-update-slice_fusion.3
  56.0 0.0 copy-done
  56.0 0.0 copy-start.10
  56.0 0.1 constant_dynamic-update-slice_fusion.2
  56.1 0.0 collective-permute-done.2
  56.1 0.1 constant_dynamic-update-slice_fusion.1
  56.2 12.0 %collective-permute-done.3 = f32[8,3,16,1024]{3,2,1,0:T(8,128)S(1)} collective-permute-done((f32[8,3,16,1024]{3,2,1,0:T(8,128)}, f32[8,3,16,1024]{3,2,1,0:T(8,128)S(1)}, u32[]{:S(2)}, u32[]{:S(2)}) %collective-permute-start.3) | collective-permute-done | bytes 1572896 | tf_op jit(solution)/shard_map/ppermute | solution.py:15
  68.2 0.1 constant_dynamic-update-slice_fusion
  68.3 0.0 copy-done.10
  68.4 0.0 copy-start.9
  68.4 4.1 %convolution_bitcast_fusion = f32[8,3,16,1024]{3,2,1,0:T(8,128)S(1)} fusion(f32[8,3,80,1024]{3,2,1,0:T(8,128)S(1)} %constant_dynamic-update-slice_fusion, f32[16]{0:T(128)S(1)} %sqrt.20, f32[16]{0:T(128)S(1)} %convert_multiply_fusion, s32[16]{0:T(128)S(1)} %copy-done.10), kind=kOutput, calls=%fused_computation.14 | convolution fusion | flops 377500160 | bytes 9437376 | tf_op jit(solution)/shard_map/ik,sckz->sciz/dot_general | solution.py:58
  72.5 0.1 fusion.44
  72.6 2.4 %collective-permute-start.4 = (f32[8,3,16,24]{3,2,1,0:T(8,128)S(1)}, f32[8,3,16,24]{3,2,1,0:T(8,128)S(1)}, u32[]{:S(2)}, u32[]{:S(2)}) collective-permute-start(f32[8,3,16,24]{3,2,1,0:T(8,128)S(1)} %get-tuple-element.19), channel_id=1, source_target_pairs={{0,1},{1,2},{2,3},{3,0},{4,5},{5,6},{6,7},{7,4},{8,9},{9,10},{10,1... | collective-permute-start | bytes 110600 | tf_op jit(solution)/shard_map/ppermute | solution.py:24
  75.0 3.6 %collective-permute-start.5 = (f32[8,3,16,24]{3,2,1,0:T(8,128)S(1)}, f32[8,3,16,24]{3,2,1,0:T(8,128)}, u32[]{:S(2)}, u32[]{:S(2)}) collective-permute-start(f32[8,3,16,24]{3,2,1,0:T(8,128)S(1)} %get-tuple-element.18), channel_id=1, source_target_pairs={{1,0},{2,1},{3,2},{0,3},{5,4},{6,5},{7,6},{4,7},{9,8},{10,9},{11,1... | collective-permute-start | bytes 110600 | tf_op jit(solution)/shard_map/ppermute | solution.py:27
  78.7 0.6 divide_exponential_fusion
  79.3 0.6 sqrt.21
  79.9 0.3 collective-permute-done.4
  80.2 3.7 %collective-permute-done.5 = f32[8,3,16,24]{3,2,1,0:T(8,128)} collective-permute-done((f32[8,3,16,24]{3,2,1,0:T(8,128)S(1)}, f32[8,3,16,24]{3,2,1,0:T(8,128)}, u32[]{:S(2)}, u32[]{:S(2)}) %collective-permute-start.5) | collective-permute-done | bytes 36896 | tf_op jit(solution)/shard_map/ppermute | solution.py:27
  83.9 1.9 %concatenate.7 = f32[8,3,16,1072]{3,2,1,0:T(8,128)S(1)} concatenate(f32[8,3,16,24]{3,2,1,0:T(8,128)S(1)} %collective-permute-done.4, f32[8,3,16,1024]{3,2,1,0:T(8,128)S(1)} %convolution_bitcast_fusion, f32[8,3,16,24]{3,2,1,0:T(8,128)} %collective-permute-done.5), dimensions={3} | concatenate | bytes 3293184 | tf_op jit(solution)/shard_map/concatenate | solution.py:28
  85.8 0.0 copy-start.2
  85.9 0.0 copy-start.6
  85.9 8.0 %fusion.3 = f32[384,1024]{1,0:T(8,128)S(1)} fusion(f32[384,1072]{1,0:T(8,128)S(1)} %bitcast.62, f32[1024]{0:T(1024)} %sqrt.21), kind=kOutput, calls=%fused_computation.4 | convolution fusion | flops 5069307904 | bytes 3223552 | tf_op jit(solution)/shard_map/rk,zk->rz/dot_general | solution.py:63
  93.9 0.0 copy-start.8
  93.9 0.1 fusion.43
  94.0 0.3 multiply_add_fusion
  94.4 0.0 copy-start.1
  94.4 0.2 copy-done.4
  94.5 0.0 copy-done.5
  94.5 0.0 copy-done.8
  94.6 0.1 multiply_add_fusion.23
  94.7 0.1 multiply_add_fusion.21
  94.8 0.1 multiply_add_fusion.19
  94.9 0.1 multiply_add_fusion.17
  95.3 0.0 copy-done.1
  95.3 0.0 copy-start.3
  95.3 1.1 %copy-done.3 = f32[8,3,16,1024]{3,2,1,0:T(8,128)} copy-done((f32[8,3,16,1024]{3,2,1,0:T(8,128)}, f32[8,3,16,1024]{3,2,1,0:T(8,128)S(1)}, u32[]{:S(2)}) %copy-start.3) | copy-done | bytes 1572888
  (16 shorter events, 0.2 us)
Async XLA Ops:
  0.6 55.3 %copy-start = (f32[8,3,16,1024]{3,2,1,0:T(8,128)S(1)}, f32[8,3,16,1024]{3,2,1,0:T(8,128)}, u32[]{:S(2)}) copy-start(f32[8,3,16,1024]{3,2,1,0:T(8,128)} %param.6) | copy-start | bytes 4718596
  0.6 39.9 %collective-permute-start = (f32[8,3,16,1024]{3,2,1,0:T(8,128)}, f32[8,3,16,1024]{3,2,1,0:T(8,128)S(1)}, u32[]{:S(2)}, u32[]{:S(2)}) collective-permute-start(f32[8,3,16,1024]{3,2,1,0:T(8,128)} %param.6), channel_id=1, source_target_pairs={{0,8},{4,12},{8,16},{12,20},{16,24},{20,28},{24,32},{28,36},{32,40... | collective-permute-start | bytes 4718600 | tf_op jit(solution)/shard_map/ppermute | solution.py:15
  5.5 50.4 %collective-permute-start.1 = (f32[8,3,16,1024]{3,2,1,0:T(8,128)}, f32[8,3,16,1024]{3,2,1,0:T(8,128)S(1)}, u32[]{:S(2)}, u32[]{:S(2)}) collective-permute-start(f32[8,3,16,1024]{3,2,1,0:T(8,128)} %param.6), channel_id=1, source_target_pairs={{0,4},{4,8},{8,12},{12,16},{16,20},{20,24},{24,28},{28,32},{32,36}... | collective-permute-start | bytes 4718600 | tf_op jit(solution)/shard_map/ppermute | solution.py:15
  7.4 48.7 %collective-permute-start.2 = (f32[8,3,16,1024]{3,2,1,0:T(8,128)}, f32[8,3,16,1024]{3,2,1,0:T(8,128)S(1)}, u32[]{:S(2)}, u32[]{:S(2)}) collective-permute-start(f32[8,3,16,1024]{3,2,1,0:T(8,128)} %param.6), channel_id=1, source_target_pairs={{4,0},{8,4},{12,8},{16,12},{20,16},{24,20},{28,24},{32,28},{36,32}... | collective-permute-start | bytes 4718600 | tf_op jit(solution)/shard_map/ppermute | solution.py:15
  11.1 57.2 %collective-permute-start.3 = (f32[8,3,16,1024]{3,2,1,0:T(8,128)}, f32[8,3,16,1024]{3,2,1,0:T(8,128)S(1)}, u32[]{:S(2)}, u32[]{:S(2)}) collective-permute-start(f32[8,3,16,1024]{3,2,1,0:T(8,128)} %param.6), channel_id=1, source_target_pairs={{8,0},{12,4},{16,8},{20,12},{24,16},{28,20},{32,24},{36,28},{40,32... | collective-permute-start | bytes 4718600 | tf_op jit(solution)/shard_map/ppermute | solution.py:15
  56.0 12.4 %copy-start.10 = (s32[16]{0:T(128)S(1)}, s32[16]{0:T(128)}, u32[]{:S(2)}) copy-start(s32[16]{0:T(128)} %param.8) | copy-start | bytes 196
  68.4 10.3 %copy-start.9 = (f32[3,16]{1,0:T(4,128)S(1)}, f32[3,16]{1,0:T(4,128)}, u32[]{:S(2)}) copy-start(f32[3,16]{1,0:T(4,128)} %param.9) | copy-start | bytes 580
  72.6 7.6 %collective-permute-start.4 = (f32[8,3,16,24]{3,2,1,0:T(8,128)S(1)}, f32[8,3,16,24]{3,2,1,0:T(8,128)S(1)}, u32[]{:S(2)}, u32[]{:S(2)}) collective-permute-start(f32[8,3,16,24]{3,2,1,0:T(8,128)S(1)} %get-tuple-element.19), channel_id=1, source_target_pairs={{0,1},{1,2},{2,3},{3,0},{4,5},{5,6},{6,7},{7,4},{8,9},{9,10},{10,1... | collective-permute-start | bytes 110600 | tf_op jit(solution)/shard_map/ppermute | solution.py:24
  75.0 8.9 %collective-permute-start.5 = (f32[8,3,16,24]{3,2,1,0:T(8,128)S(1)}, f32[8,3,16,24]{3,2,1,0:T(8,128)}, u32[]{:S(2)}, u32[]{:S(2)}) collective-permute-start(f32[8,3,16,24]{3,2,1,0:T(8,128)S(1)} %get-tuple-element.18), channel_id=1, source_target_pairs={{1,0},{2,1},{3,2},{0,3},{5,4},{6,5},{7,6},{4,7},{9,8},{10,9},{11,1... | collective-permute-start | bytes 110600 | tf_op jit(solution)/shard_map/ppermute | solution.py:27
  85.8 8.2 %copy-start.2 = (f32[3,16,1024]{2,1,0:T(8,128)S(1)}, f32[3,16,1024]{2,1,0:T(8,128)}, u32[]{:S(2)}) copy-start(f32[3,16,1024]{2,1,0:T(8,128)} %param.7) | copy-start | bytes 589828
  85.9 8.2 %copy-start.6 = (f32[3,16]{1,0:T(4,128)S(1)}, f32[3,16]{1,0:T(4,128)}, u32[]{:S(2)}) copy-start(f32[3,16]{1,0:T(4,128)} %get-tuple-element.62) | copy-start | bytes 580
  85.9 8.2 %copy-start.7 = (f32[3,16]{1,0:T(4,128)S(1)}, f32[3,16]{1,0:T(4,128)}, u32[]{:S(2)}) copy-start(f32[3,16]{1,0:T(4,128)} %get-tuple-element.63) | copy-start | bytes 580
  93.9 0.7 copy-start.4
  93.9 0.7 copy-start.5
  93.9 0.7 copy-start.8
  94.4 0.9 copy-start.1
  95.3 1.1 %copy-start.3 = (f32[8,3,16,1024]{3,2,1,0:T(8,128)}, f32[8,3,16,1024]{3,2,1,0:T(8,128)S(1)}, u32[]{:S(2)}) copy-start(f32[8,3,16,1024]{3,2,1,0:T(8,128)S(1)} %fusion.19) | copy-start | bytes 4718596
where the time goes:
time: 96.8 us; the launch traced here: 96.4 us
  waiting for transfers between devices  54.6 us (56%)
  starting transfers between devices  18.3 us (19%)
  matrix products  12.1 us (12%)
  local copies, waits for them, and re-layouts  6.13 us (6%)
  other arithmetic  4.23 us (4%)
  between operations  1 us (1%)
    ppermute x4, waiting for transfers between devices, shifted(): return lax.ppermute(shard, axis, pairs)  50.6 us
    ppermute x4, starting transfers between devices, shifted(): return lax.ppermute(shard, axis, pairs)  12.3 us
    dot_general x1, matrix products, shards(): jnp.einsum('rk,zk->rz', flat_margin, span_band, precision=highest)  7.99 us
    dot_general x1, matrix products, shards(): jnp.einsum('ik,sckz->sciz', wall_band, extended, precision=highest)  4.14 us
    ppermute x1, waiting for transfers between devices, with_halo(): lax.ppermute(lax.slice_in_dim(block, 0, width, axis=dim), axis, backward)  3.71 us
    ppermute x1, starting transfers between devices, with_halo(): lax.ppermute(lax.slice_in_dim(block, 0, width, axis=dim), axis, backward)  3.64 us
    ppermute x1, starting transfers between devices, with_halo(): lax.ppermute(lax.slice_in_dim(block, block.shape[dim] - width, None, axis...  2.39 us
    reduce_sum x2, other arithmetic, band_matrix(): return shaped / jnp.sqrt(jnp.sum(shaped * shaped, axis=1, keepdims=True))  2.03 us
  transfers between devices with their start and end apart: 6, of which 5 were waited for; matrix products, arithmetic and copies ran while one was open for 6% of the time, Pallas kernels for 0%

commit v1 on v0

v1 whole, which is shorter than its diff:
```python
import math

import jax
import jax.numpy as jnp
import numpy as np
from jax import lax
from jax.experimental import pallas as pl
from jax.experimental.pallas import tpu as pltpu
from jax.sharding import PartitionSpec as P


HMAX = 32
HZ = 24
LANES = 128
TILE = 256
EDGE = 32
VMEM_BYTES = 16 * 2**20

f32 = jnp.float32
bf16 = jnp.bfloat16


def span_band():
    offsets = np.arange(-HZ, HZ + 1, dtype=np.float64)
    raw = np.exp(-2.0 * np.pi * offsets**2 / HZ**2)
    unit = raw / np.sqrt(np.sum(raw * raw))
    rows = np.arange(TILE + 2 * LANES)[:, None]
    cols = np.arange(TILE)[None, :]
    j = rows - LANES - cols
    band = np.where(np.abs(j) <= HZ, unit[np.clip(j + HZ, 0, 2 * HZ)], 0.0).astype(np.float32)
    high = band.astype(jnp.bfloat16)
    low = (band - high.astype(np.float32)).astype(jnp.bfloat16)
    return np.stack([high, low])


def halves(x):
    high = x.astype(bf16)
    return high, (x - high.astype(f32)).astype(bf16)


def dot(a, b):
    return jnp.dot(a, b, preferred_element_type=f32)


def spread(packed, last):
    pieces = []
    for group in range(LANES // EDGE):
        shift = (LANES - EDGE if last else 0) - group * EDGE
        pieces.append(pltpu.roll(packed, shift % LANES, 1) if shift else packed)
    return jnp.concatenate(pieces, axis=0)


def gathered(edge, last):
    count = edge.shape[0] // (LANES // EDGE)
    lane = lax.broadcasted_iota(jnp.int32, (count, LANES), 1) // EDGE
    total = jnp.zeros((count, LANES), f32)
    for group in range(LANES // EDGE):
        piece = edge[group * count : (group + 1) * count]
        shift = group * EDGE - (LANES - EDGE if last else 0)
        total = jnp.where(lane == group, pltpu.roll(piece, shift % LANES, 1) if shift else piece, total)
    return total


def pack_kernel(first_ref, last_ref, right_ref, left_ref):
    right_ref[...] = gathered(first_ref[...], False)
    left_ref[...] = gathered(last_ref[...], True)


def fill_window(x_ref, left, right, high_ref, low_ref):
    width = x_ref.shape[1]
    high_ref[:, :LANES], low_ref[:, :LANES] = halves(spread(left, True))
    high_ref[:, LANES : LANES + width], low_ref[:, LANES : LANES + width] = halves(x_ref[...])
    high_ref[:, LANES + width :], low_ref[:, LANES + width :] = halves(spread(right, False))


def span_filter(high_ref, low_ref, band_ref, store):
    width = high_ref.shape[1] - 2 * LANES
    for start in range(0, width, TILE):
        window = pl.ds(start, TILE + 2 * LANES)
        high = high_ref[:, window]
        low = low_ref[:, window]
        store(
            pl.ds(start, TILE),
            dot(high, band_ref[0]) + dot(low, band_ref[0]) + dot(high, band_ref[1]),
        )


def own_kernel(x_ref, left_ref, right_ref, band_ref, out_ref, edge_ref, high_ref, low_ref):
    fill_window(x_ref, left_ref[...], right_ref[...], high_ref, low_ref)
    count = left_ref.shape[0]
    edge_ref[:count, :] = left_ref[...]
    edge_ref[count:, :] = right_ref[...]

    def store(columns, value):
        out_ref[:, columns] = value

    span_filter(high_ref, low_ref, band_ref, store)


def wall_kernel(
    own_ref, far_ref, edge_ref, band_ref, weight_ref, mine_ref, theirs_ref,
    high_ref, low_ref, far_high_ref, far_low_ref,
):
    count = edge_ref.shape[0] // 2
    fill_window(far_ref, edge_ref[:count, :], edge_ref[count:, :], high_ref, low_ref)

    def store(columns, value):
        far_high_ref[:, columns], far_low_ref[:, columns] = halves(value)

    span_filter(high_ref, low_ref, band_ref, store)
    rows = weight_ref.shape[0] // 2
    planes = own_ref.shape[0] // rows
    group = 6

    def some_planes(index, carry):
        for one in range(group):
            at = pl.ds(pl.multiple_of((index * group + one) * rows, rows), rows)
            own_high, own_low = halves(own_ref[at, :])
            high = [own_high, far_high_ref[at, :]]
            low = [own_low, far_low_ref[at, :]]
            both = dot(weight_ref[...], jnp.concatenate(high + low + high, axis=0))
            mine_ref[at, :] = both[:rows]
            theirs_ref[at, :] = both[rows:]
        return carry

    lax.fori_loop(0, planes // group, some_planes, 0)


def step_kernel(
    mine_ref, theirs_ref, near_ref, weight_ref, row_ref, previous_ref, velocity_ref, state_ref,
    made_ref, field_ref, sems,
):
    rows = weight_ref.shape[0]
    repeat = previous_ref.shape[1] // LANES
    steps = made_ref.shape[0] // (3 * rows)

    def row(index):
        return jnp.concatenate([row_ref[index]] * repeat, axis=1)

    copies = []
    for step in range(steps):
        field = []
        for part in range(3):
            at = pl.ds((step * 3 + part) * rows, rows)
            of = pl.ds(part * rows, rows)
            high, low = halves(near_ref[at, :])
            total = mine_ref[at, :] + theirs_ref[at, :]
            total = total + dot(weight_ref[...], jnp.concatenate([high, low, high], axis=0))
            before = previous_ref[of, :] if step == 0 else field_ref[of, :]
            now = row(part) * before + row(3 + part) * total
            field_ref[of, :] = now
            field.append(now)
        at = step * 3 * rows
        made_ref[pl.ds(at, rows), :] = row(12) + row(6) * field[0]
        made_ref[pl.ds(at + rows, rows), :] = row(7) * field[0] + row(8) * field[1]
        made_ref[pl.ds(at + 2 * rows, rows), :] = (
            row(9) * field[0] + row(10) * field[1] + row(11) * field[2]
        )
        block = pl.ds(at, 3 * rows)
        copy = pltpu.make_async_copy(made_ref.at[block], velocity_ref.at[block], sems.at[step])
        copy.start()
        copies.append(copy)
    copy = pltpu.make_async_copy(field_ref, state_ref, sems.at[steps])
    copy.start()
    for one in copies + [copy]:
        one.wait()


WHOLE = pl.BlockSpec(memory_space=pltpu.VMEM)


def vmem(x):
    return pltpu.with_memory_space_constraint(x, pltpu.VMEM)


def hbm(x):
    return pltpu.with_memory_space_constraint(x, pltpu.HBM)


def call(kernel, out, scratch, flops, *args, in_specs=None, out_specs=WHOLE, **more):
    moved = sum(a.size * a.dtype.itemsize for a in args)
    return pl.pallas_call(
        kernel,
        out_shape=out,
        in_specs=in_specs or [WHOLE] * len(args),
        out_specs=jax.tree.map(lambda _: out_specs, out),
        scratch_shapes=scratch,
        cost_estimate=pl.CostEstimate(flops=flops, bytes_accessed=moved, transcendentals=0),
        compiler_params=pltpu.CompilerParams(vmem_limit_bytes=VMEM_BYTES),
        **more,
    )(*args)


def wall_weights(widths, *starts):
    count = widths.shape[0]
    spread = widths.astype(f32)[:, None]

    def raw(offset):
        distance = offset.astype(f32)
        return jnp.where(
            jnp.abs(offset) <= widths[:, None],
            jnp.exp(-2.0 * math.pi * distance * distance / (spread * spread)),
            0.0,
        )

    every = raw(lax.broadcasted_iota(jnp.int32, (count, 2 * HMAX + 1), 1) - HMAX)
    size = jnp.sqrt(jnp.sum(every * every, axis=1, keepdims=True))
    row = lax.broadcasted_iota(jnp.int32, (count, count), 0)
    col = lax.broadcasted_iota(jnp.int32, (count, count), 1)
    return [raw(col - row + start) / size for start in starts]


def split3(weights):
    high = lax.reduce_precision(weights, exponent_bits=8, mantissa_bits=7)
    low = lax.reduce_precision(weights - high, exponent_bits=8, mantissa_bits=7)
    return jnp.concatenate([high, high, low], axis=1).astype(bf16)


def planes(random_planes, previous, half_width, time_scale, lund_factor, mean_velocity):
    steps, parts, rows, width = random_planes.shape
    wall = lax.axis_size("wall")
    span = lax.axis_size("span")
    core = lax.axis_index("wall") % 2
    sign = 1 - 2 * core
    near_pairs = []
    far_pairs = []
    for at in range(wall):
        way = 2 - 4 * (at % 2)
        if 0 <= at - way < wall:
            near_pairs.append((at - way, at))
        if 0 <= at + way < wall:
            far_pairs.append((at + way, at))
    swap = [(at, at ^ 1) for at in range(wall)]
    forward = [(i, (i + 1) % span) for i in range(span)]
    backward = [(target, source) for source, target in forward]

    x = random_planes.reshape(steps * parts * rows, width)
    count = x.shape[0]
    packed_rows = count * EDGE // LANES
    far = lax.ppermute(x, "wall", far_pairs)
    packed = pltpu.VMEM((packed_rows, LANES), f32)
    mine_right, mine_left = call(
        pack_kernel, (packed, packed), [], 0, hbm(x), hbm(x),
        in_specs=[
            pl.BlockSpec((count, LANES), lambda i: (0, 0)),
            pl.BlockSpec((count, LANES), lambda i: (0, width // LANES - 1)),
        ],
        grid=(1,),
    )
    left = lax.ppermute(mine_left, "span", forward)
    right = lax.ppermute(mine_right, "span", backward)

    band = jnp.asarray(span_band())
    block = pltpu.VMEM(x.shape, f32)
    window = pltpu.VMEM((count, width + 2 * LANES), bf16)
    inner = pltpu.VMEM((count, width), bf16)
    span_flops = 2 * count * width * 512 * 3
    wall_flops = 2 * count * width * 32 * 6
    own, far_edges = call(
        own_kernel, (block, pltpu.VMEM((2 * packed_rows, LANES), f32)), [window] * 2,
        span_flops, vmem(x), vmem(left), vmem(right), vmem(band),
    )
    near = lax.ppermute(own, "wall", near_pairs)
    far_edges = lax.ppermute(far_edges, "wall", far_pairs)
    other_width = lax.ppermute(half_width, "wall", swap)

    own_w, far_w, near_w = wall_weights(half_width, 0, 2 * rows * sign, -2 * rows * sign)
    own_o, far_o = wall_weights(other_width, -rows * sign, rows * sign)
    both = split3(jnp.concatenate(
        [jnp.concatenate([own_w, far_w], axis=1), jnp.concatenate([own_o, far_o], axis=1)],
        axis=0,
    ))
    near_w = split3(near_w)
    retain = jnp.exp(-math.pi / (2.0 * time_scale))
    inject = jnp.sqrt(1.0 - jnp.exp(-math.pi / time_scale))
    per_row = jnp.concatenate([retain, inject, lund_factor, mean_velocity[None]], axis=0)
    per_row = jnp.broadcast_to(per_row[:, :, None], per_row.shape + (LANES,))
    mine, theirs = call(
        wall_kernel, (block, block), [window] * 2 + [inner] * 2,
        span_flops + wall_flops, vmem(own), vmem(far), vmem(far_edges), vmem(band), vmem(both),
    )
    theirs = lax.ppermute(theirs, "wall", swap)
    velocity, state = call(
        step_kernel,
        (jax.ShapeDtypeStruct(x.shape, f32), jax.ShapeDtypeStruct((parts * rows, width), f32)),
        [
            pltpu.VMEM(x.shape, f32), pltpu.VMEM((parts * rows, width), f32),
            pltpu.SemaphoreType.DMA((steps + 1,)),
        ],
        wall_flops, vmem(mine), vmem(theirs), vmem(near), vmem(near_w), vmem(per_row),
        vmem(previous.reshape(parts * rows, width)),
        out_specs=pl.BlockSpec(memory_space=pl.ANY),
    )
    return velocity.reshape(random_planes.shape), state.reshape(previous.shape)


def solution(mesh):
    in_specs = (
        P(None, None, "wall", "span"),
        P(None, "wall", "span"),
        P("wall"),
        P(None, "wall"),
        P(None, "wall"),
        P("wall"),
    )
    out_specs = (P(None, None, "wall", "span"), P(None, "wall", "span"))
    return jax.shard_map(planes, mesh=mesh, in_specs=in_specs, out_specs=out_specs, check_vma=False)
```

time: 96.8 us -> 52.7 us (0.54)
  the two profiles are of different devices: /device:TPU:254 before, /device:TPU:262 now
where the time goes in v1:
time: 52.7 us; the launch traced here: 52.3 us
  waiting for transfers between devices  21.6 us (41%)
  starting transfers between devices  21.2 us (40%)
  Pallas kernels  6.94 us (13%)
  local copies, waits for them, and re-layouts  1.16 us (2%)
  between operations  0.86 us (2%)
  other arithmetic  0.58 us (1%)
    ppermute x1, waiting for transfers between devices, planes(): near = lax.ppermute(own, 'wall', near_pairs)  17.4 us
    pallas_call x4, Pallas kernels, call(): pl.pallas_call(kernel, out_shape=out, in_specs=in_specs or [WHOLE] * len(...  6.94 us
    ppermute x1, starting transfers between devices, planes(): far = lax.ppermute(x, 'wall', far_pairs)  4.6 us
    ppermute x1, starting transfers between devices, planes(): far_edges = lax.ppermute(far_edges, 'wall', far_pairs)  4.24 us
    ppermute x1, starting transfers between devices, planes(): right = lax.ppermute(mine_right, 'span', backward)  3.46 us
    ppermute x1, waiting for transfers between devices, planes(): right = lax.ppermute(mine_right, 'span', backward)  3.24 us
    ppermute x1, starting transfers between devices, planes(): theirs = lax.ppermute(theirs, 'wall', swap)  2.56 us
    ppermute x1, starting transfers between devices, planes(): left = lax.ppermute(mine_left, 'span', forward)  2.39 us
  transfers between devices with their start and end apart: 7, of which 3 were waited for; matrix products, arithmetic and copies ran while one was open for 1% of the time, Pallas kernels for 10%

profile of v1, /device:TPU:262, one launch (start us, length us, event | category | flops | bytes accessed | tf_op | source)
XLA Modules:
  0.0 52.3 jit_solution(17130353775403219133)
XLA Ops:
  0.6 0.0 copy-start.5
  0.6 0.0 copy-start
  0.6 4.6 %collective-permute-start.2 = (f32[384,1024]{1,0:T(8,128)}, f32[384,1024]{1,0:T(8,128)S(1)}, u32[]{:S(2)}, u32[]{:S(2)}) collective-permute-start(f32[384,1024]{1,0:T(8,128)} %bitcast.5), channel_id=1, source_target_pairs={{8,0},{16,8},{4,12},{24,16},{12,20},{32,24},{20,28},{40,32},{28,36... | collective-permute-start | bytes 4718600 | tf_op jit(solution)/shard_map/ppermute | solution.py:240
  5.3 1.9 %collective-permute-start.4 = (s32[16]{0:T(128)}, s32[16]{0:T(128)S(1)}, u32[]{:S(2)}, u32[]{:S(2)}) collective-permute-start(s32[16]{0:T(128)} %param.9), channel_id=1, source_target_pairs={{0,4},{4,0},{8,12},{12,8},{16,20},{20,16},{24,28},{28,24},{32,36},... | collective-permute-start | bytes 200 | tf_op jit(solution)/shard_map/ppermute | solution.py:265
  7.2 1.2 %shard_map.86 = (f32[96,128]{1,0:T(8,128)S(1)}, f32[96,128]{1,0:T(8,128)S(1)}) custom-call(f32[384,1024]{1,0:T(8,128)} %bitcast.6, f32[384,1024]{1,0:T(8,128)} %bitcast.7), custom_call_target="tpu_custom_call" | custom-call | bytes 3145728 | tf_op jit(solution)/shard_map/pallas_call | solution.py:182
  8.4 2.4 %collective-permute-start = (f32[96,128]{1,0:T(8,128)S(1)}, f32[96,128]{1,0:T(8,128)S(1)}, u32[]{:S(2)}, u32[]{:S(2)}) collective-permute-start(f32[96,128]{1,0:T(8,128)S(1)} %get-tuple-element.10), channel_id=1, source_target_pairs={{0,1},{1,2},{2,3},{3,0},{4,5},{5,6},{6,7},{7,4},{8,9},{9,10},{10,1... | collective-permute-start | bytes 147464 | tf_op jit(solution)/shard_map/ppermute | solution.py:250
  10.8 3.5 %collective-permute-start.1 = (f32[96,128]{1,0:T(8,128)S(1)}, f32[96,128]{1,0:T(8,128)S(1)}, u32[]{:S(2)}, u32[]{:S(2)}) collective-permute-start(f32[96,128]{1,0:T(8,128)S(1)} %get-tuple-element.11), channel_id=1, source_target_pairs={{1,0},{2,1},{3,2},{0,3},{5,4},{6,5},{7,6},{4,7},{9,8},{10,9},{11,1... | collective-permute-start | bytes 147464 | tf_op jit(solution)/shard_map/ppermute | solution.py:251
  14.3 0.0 copy-done.5
  14.3 0.0 collective-permute-done.4
  14.3 0.2 fusion.28
  14.5 0.1 reduce-precision_convert_fusion.1
  14.6 0.1 reduce-precision_convert_fusion
  14.7 0.0 collective-permute-done.left_ref
  14.7 3.2 %collective-permute-done.1.right_ref = f32[96,128]{1,0:T(8,128)S(1)} collective-permute-done((f32[96,128]{1,0:T(8,128)S(1)}, f32[96,128]{1,0:T(8,128)S(1)}, u32[]{:S(2)}, u32[]{:S(2)}) %collective-permute-start.1) | collective-permute-done | bytes 49184 | tf_op jit(solution)/shard_map/ppermute | solution.py:251
  17.9 0.0 copy-done
  17.9 0.0 copy-start.2
  17.9 1.0 %copy-done.2 = bf16[2,512,256]{2,1,0:T(8,128)(2,1)S(1)} copy-done((bf16[2,512,256]{2,1,0:T(8,128)(2,1)S(1)}, bf16[2,512,256]{2,1,0:T(8,128)(2,1)}, u32[]{:S(2)}) %copy-start.2) | copy-done | bytes 524312
  19.0 0.0 copy-start.3
  19.0 1.5 %shard_map.87 = (f32[384,1024]{1,0:T(8,128)S(1)}, f32[192,128]{1,0:T(8,128)S(1)}) custom-call(f32[384,1024]{1,0:T(8,128)S(1)} %bitcast.8, f32[96,128]{1,0:T(8,128)S(1)} %collective-permute-done.left_ref, f32[96,128]{1,0:T(8,128)S(1)} %collective-permute-done.1.right_ref, bf16[2,512,256]{2,1,0:T(8,128)(2,1)S(1)} %copy-done.2), custom_call_target="tpu_custom_call" | custom-call | flops 1207959552 | bytes 2195456 | tf_op jit(solution)/shard_map/pallas_call | solution.py:182
  20.5 4.2 %collective-permute-start.3 = (f32[192,128]{1,0:T(8,128)S(1)}, f32[192,128]{1,0:T(8,128)S(1)}, u32[]{:S(2)}, u32[]{:S(2)}) collective-permute-start(f32[192,128]{1,0:T(8,128)S(1)} %get-tuple-element.13), channel_id=1, source_target_pairs={{8,0},{16,8},{4,12},{24,16},{12,20},{32,24},{20,28},{40,32},{28,36... | collective-permute-start | bytes 294920 | tf_op jit(solution)/shard_map/ppermute | solution.py:264
  24.7 0.1 pad_maximum_fusion.weight_ref
  24.8 0.0 copy-start.6
  24.8 0.0 copy-start.4
  24.8 0.0 copy-start.7
  24.8 0.0 copy-start.1
  24.8 2.1 %collective-permute-start.6 = (f32[384,1024]{1,0:T(8,128)S(1)}, f32[384,1024]{1,0:T(8,128)S(1)}, u32[]{:S(2)}, u32[]{:S(2)}) collective-permute-start(f32[384,1024]{1,0:T(8,128)S(1)} %get-tuple-element.12.own_ref), channel_id=1, source_target_pairs={{12,4},{0,8},{20,12},{8,16},{28,20},{16,24},{36,28},{24,32},{44,36... | collective-permute-start | bytes 4718600 | tf_op jit(solution)/shard_map/ppermute | solution.py:263
  26.9 0.9 %collective-permute-done.3.edge_ref = f32[192,128]{1,0:T(8,128)S(1)} collective-permute-done((f32[192,128]{1,0:T(8,128)S(1)}, f32[192,128]{1,0:T(8,128)S(1)}, u32[]{:S(2)}, u32[]{:S(2)}) %collective-permute-start.3) | collective-permute-done | bytes 98336 | tf_op jit(solution)/shard_map/ppermute | solution.py:264
  27.8 0.0 collective-permute-done.2.far_ref
  27.8 0.0 copy-done.3
  27.8 2.7 %shard_map.88 = (f32[384,1024]{1,0:T(8,128)S(1)}, f32[384,1024]{1,0:T(8,128)S(1)}) custom-call(f32[384,1024]{1,0:T(8,128)S(1)} %get-tuple-element.12.own_ref, f32[384,1024]{1,0:T(8,128)S(1)} %collective-permute-done.2.far_ref, f32[192,128]{1,0:T(8,128)S(1)} %collective-permute-done.3.edge_ref, bf16[2,512,256]{2,1,0:T(8,128)(2,1)S(1)} %copy-done.3, ...), custom_call_target="tpu_custom_call" | custom-call | flops 1358954496 | bytes 3774464 | tf_op jit(solution)/shard_map/pallas_call | solution.py:182
  30.4 2.6 %collective-permute-start.5 = (f32[384,1024]{1,0:T(8,128)S(1)}, f32[384,1024]{1,0:T(8,128)S(1)}, u32[]{:S(2)}, u32[]{:S(2)}) collective-permute-start(f32[384,1024]{1,0:T(8,128)S(1)} %get-tuple-element.15), channel_id=1, source_target_pairs={{0,4},{4,0},{8,12},{12,8},{16,20},{20,16},{24,28},{28,24},{32,36},... | collective-permute-start | bytes 4718600 | tf_op jit(solution)/shard_map/ppermute | solution.py:282
  33.0 0.0 copy-done.6
  33.0 0.0 copy-done.4
  33.0 0.0 copy-done.7
  33.0 0.1 pad_maximum_fusion.2.weight_ref
  33.1 17.4 %collective-permute-done.6.near_ref = f32[384,1024]{1,0:T(8,128)S(1)} collective-permute-done((f32[384,1024]{1,0:T(8,128)S(1)}, f32[384,1024]{1,0:T(8,128)S(1)}, u32[]{:S(2)}, u32[]{:S(2)}) %collective-permute-start.6) | collective-permute-done | bytes 1572896 | tf_op jit(solution)/shard_map/ppermute | solution.py:263
  50.6 0.0 collective-permute-done.5.theirs_ref
  50.6 0.1 broadcast_in_dim.36.row_ref
  50.7 0.0 copy-done.1
  50.7 1.7 %shard_map.89 = (f32[384,1024]{1,0:T(8,128)}, f32[48,1024]{1,0:T(8,128)}) custom-call(f32[384,1024]{1,0:T(8,128)S(1)} %get-tuple-element.14.mine_ref, f32[384,1024]{1,0:T(8,128)S(1)} %collective-permute-done.5.theirs_ref, f32[384,1024]{1,0:T(8,128)S(1)} %collective-permute-done.6.near_ref, bf16[16,48]{1,0:T(8,128)(2,1)S(1)} %pad_maximum_fusion.2.weight_ref, ...), custom_call_target="tpu_custom_call" | custom-call | flops 150994944 | bytes 5023232 | tf_op jit(solution)/shard_map/pallas_call | solution.py:182
  (8 shorter events, 0.1 us)
Async XLA Ops:
  0.6 13.6 %copy-start.5 = (s32[16]{0:T(128)S(1)}, s32[16]{0:T(128)}, u32[]{:S(2)}) copy-start(s32[16]{0:T(128)} %param.9) | copy-start | bytes 196
  0.6 17.3 %copy-start = (f32[8,3,16,1024]{3,2,1,0:T(8,128)S(1)}, f32[8,3,16,1024]{3,2,1,0:T(8,128)}, u32[]{:S(2)}) copy-start(f32[8,3,16,1024]{3,2,1,0:T(8,128)} %param.7) | copy-start | bytes 4718596
  0.6 27.1 %collective-permute-start.2 = (f32[384,1024]{1,0:T(8,128)}, f32[384,1024]{1,0:T(8,128)S(1)}, u32[]{:S(2)}, u32[]{:S(2)}) collective-permute-start(f32[384,1024]{1,0:T(8,128)} %bitcast.5), channel_id=1, source_target_pairs={{8,0},{16,8},{4,12},{24,16},{12,20},{32,24},{20,28},{40,32},{28,36... | collective-permute-start | bytes 4718600 | tf_op jit(solution)/shard_map/ppermute | solution.py:240
  5.3 9.0 %collective-permute-start.4 = (s32[16]{0:T(128)}, s32[16]{0:T(128)S(1)}, u32[]{:S(2)}, u32[]{:S(2)}) collective-permute-start(s32[16]{0:T(128)} %param.9), channel_id=1, source_target_pairs={{0,4},{4,0},{8,12},{12,8},{16,20},{20,16},{24,28},{28,24},{32,36},... | collective-permute-start | bytes 200 | tf_op jit(solution)/shard_map/ppermute | solution.py:265
  8.4 6.3 %collective-permute-start = (f32[96,128]{1,0:T(8,128)S(1)}, f32[96,128]{1,0:T(8,128)S(1)}, u32[]{:S(2)}, u32[]{:S(2)}) collective-permute-start(f32[96,128]{1,0:T(8,128)S(1)} %get-tuple-element.10), channel_id=1, source_target_pairs={{0,1},{1,2},{2,3},{3,0},{4,5},{5,6},{6,7},{7,4},{8,9},{9,10},{10,1... | collective-permute-start | bytes 147464 | tf_op jit(solution)/shard_map/ppermute | solution.py:250
  10.8 7.2 %collective-permute-start.1 = (f32[96,128]{1,0:T(8,128)S(1)}, f32[96,128]{1,0:T(8,128)S(1)}, u32[]{:S(2)}, u32[]{:S(2)}) collective-permute-start(f32[96,128]{1,0:T(8,128)S(1)} %get-tuple-element.11), channel_id=1, source_target_pairs={{1,0},{2,1},{3,2},{0,3},{5,4},{6,5},{7,6},{4,7},{9,8},{10,9},{11,1... | collective-permute-start | bytes 147464 | tf_op jit(solution)/shard_map/ppermute | solution.py:251
  17.9 1.0 %copy-start.2 = (bf16[2,512,256]{2,1,0:T(8,128)(2,1)S(1)}, bf16[2,512,256]{2,1,0:T(8,128)(2,1)}, u32[]{:S(2)}) copy-start(bf16[2,512,256]{2,1,0:T(8,128)(2,1)} %constant.43.clone.band_ref) | copy-start | bytes 1572868
  19.0 8.8 %copy-start.3 = (bf16[2,512,256]{2,1,0:T(8,128)(2,1)S(1)}, bf16[2,512,256]{2,1,0:T(8,128)(2,1)}, u32[]{:S(2)}) copy-start(bf16[2,512,256]{2,1,0:T(8,128)(2,1)} %constant.43.clone.band_ref) | copy-start | bytes 1572868
  20.5 7.3 %collective-permute-start.3 = (f32[192,128]{1,0:T(8,128)S(1)}, f32[192,128]{1,0:T(8,128)S(1)}, u32[]{:S(2)}, u32[]{:S(2)}) collective-permute-start(f32[192,128]{1,0:T(8,128)S(1)} %get-tuple-element.13), channel_id=1, source_target_pairs={{8,0},{16,8},{4,12},{24,16},{12,20},{32,24},{20,28},{40,32},{28,36... | collective-permute-start | bytes 294920 | tf_op jit(solution)/shard_map/ppermute | solution.py:264
  24.8 8.2 %copy-start.6 = (f32[3,16]{1,0:T(4,128)S(1)}, f32[3,16]{1,0:T(4,128)}, u32[]{:S(2)}) copy-start(f32[3,16]{1,0:T(4,128)} %param.10) | copy-start | bytes 580
  24.8 8.2 %copy-start.4 = (f32[6,16]{1,0:T(8,128)S(1)}, f32[6,16]{1,0:T(8,128)}, u32[]{:S(2)}) copy-start(f32[6,16]{1,0:T(8,128)} %param.11) | copy-start | bytes 1156
  24.8 8.2 %copy-start.7 = (f32[16]{0:T(128)S(1)}, f32[16]{0:T(128)}, u32[]{:S(2)}) copy-start(f32[16]{0:T(128)} %param.12) | copy-start | bytes 196
  24.8 25.9 %copy-start.1 = (f32[3,16,1024]{2,1,0:T(8,128)S(1)}, f32[3,16,1024]{2,1,0:T(8,128)}, u32[]{:S(2)}) copy-start(f32[3,16,1024]{2,1,0:T(8,128)} %param.8) | copy-start | bytes 589828
  24.8 25.8 %collective-permute-start.6 = (f32[384,1024]{1,0:T(8,128)S(1)}, f32[384,1024]{1,0:T(8,128)S(1)}, u32[]{:S(2)}, u32[]{:S(2)}) collective-permute-start(f32[384,1024]{1,0:T(8,128)S(1)} %get-tuple-element.12.own_ref), channel_id=1, source_target_pairs={{12,4},{0,8},{20,12},{8,16},{28,20},{16,24},{36,28},{24,32},{44,36... | collective-permute-start | bytes 4718600 | tf_op jit(solution)/shard_map/ppermute | solution.py:263
  30.4 20.2 %collective-permute-start.5 = (f32[384,1024]{1,0:T(8,128)S(1)}, f32[384,1024]{1,0:T(8,128)S(1)}, u32[]{:S(2)}, u32[]{:S(2)}) collective-permute-start(f32[384,1024]{1,0:T(8,128)S(1)} %get-tuple-element.15), channel_id=1, source_target_pairs={{0,4},{4,0},{8,12},{12,8},{16,20},{20,16},{24,28},{28,24},{32,36},... | collective-permute-start | bytes 4718600 | tf_op jit(solution)/shard_map/ppermute | solution.py:282

commit v2 on v1

v2 whole, which is shorter than its diff:
```python
import math

import jax
import jax.numpy as jnp
import numpy as np
from jax import lax
from jax.experimental import pallas as pl
from jax.experimental.pallas import tpu as pltpu
from jax.sharding import PartitionSpec as P


HMAX = 32
HZ = 24
LANES = 128
TILE = 256
EDGE = 32
LAST_STEPS = 2
VMEM_BYTES = 16 * 2**20

f32 = jnp.float32
bf16 = jnp.bfloat16


def span_band():
    offsets = np.arange(-HZ, HZ + 1, dtype=np.float64)
    raw = np.exp(-2.0 * np.pi * offsets**2 / HZ**2)
    unit = raw / np.sqrt(np.sum(raw * raw))
    rows = np.arange(TILE + 2 * LANES)[:, None]
    cols = np.arange(TILE)[None, :]
    j = rows - LANES - cols
    band = np.where(np.abs(j) <= HZ, unit[np.clip(j + HZ, 0, 2 * HZ)], 0.0).astype(np.float32)
    high = band.astype(jnp.bfloat16)
    low = (band - high.astype(np.float32)).astype(jnp.bfloat16)
    return np.stack([high, low])


def halves(x):
    high = x.astype(bf16)
    return high, (x - high.astype(f32)).astype(bf16)


def dot(a, b):
    return jnp.dot(a, b, preferred_element_type=f32)


def spread(packed, last):
    pieces = []
    for group in range(LANES // EDGE):
        shift = (LANES - EDGE if last else 0) - group * EDGE
        pieces.append(pltpu.roll(packed, shift % LANES, 1) if shift else packed)
    return jnp.concatenate(pieces, axis=0)


def gathered(edge, last):
    count = edge.shape[0] // (LANES // EDGE)
    lane = lax.broadcasted_iota(jnp.int32, (count, LANES), 1) // EDGE
    total = jnp.zeros((count, LANES), f32)
    for group in range(LANES // EDGE):
        piece = edge[group * count : (group + 1) * count]
        shift = group * EDGE - (LANES - EDGE if last else 0)
        total = jnp.where(lane == group, pltpu.roll(piece, shift % LANES, 1) if shift else piece, total)
    return total


def pack_kernel(first_ref, last_ref, right_ref, left_ref):
    right_ref[...] = gathered(first_ref[...], False)
    left_ref[...] = gathered(last_ref[...], True)


def put(high_ref, low_ref, start, value):
    at = pl.ds(start, value.shape[1])
    high_ref[:, at], low_ref[:, at] = halves(value)


def fill_inner(x_ref, high_ref, low_ref):
    width = x_ref.shape[1]
    put(high_ref, low_ref, 0, x_ref[:, TILE - LANES : width - TILE + LANES])


def fill_outer(x_ref, left, right, high_ref, low_ref):
    own = TILE + LANES
    put(high_ref, low_ref, 0, spread(left, True))
    put(high_ref, low_ref, LANES, x_ref[:, :own])
    put(high_ref, low_ref, LANES + own, x_ref[:, x_ref.shape[1] - own :])
    put(high_ref, low_ref, LANES + 2 * own, spread(right, False))


def filtered(high_ref, low_ref, band_ref, start):
    window = pl.ds(start, TILE + 2 * LANES)
    high = high_ref[:, window]
    return (
        dot(high, band_ref[0]) + dot(low_ref[:, window], band_ref[0]) + dot(high, band_ref[1])
    )


def own_inner_kernel(x_ref, band_hbm, out_ref, band_ref, high_ref, low_ref, sem):
    copy = pltpu.make_async_copy(band_hbm, band_ref, sem)
    copy.start()
    fill_inner(x_ref, high_ref, low_ref)
    copy.wait()
    for at in range(TILE, x_ref.shape[1] - TILE, TILE):
        out_ref[:, at - TILE : at] = filtered(high_ref, low_ref, band_ref, at - TILE)


def own_outer_kernel(
    inner_ref, x_ref, left_ref, right_ref, band_ref, first_ref, last_ref, edge_ref,
    high_ref, low_ref,
):
    count = left_ref.shape[0]
    edge_ref[:count, :] = left_ref[...]
    edge_ref[count:, :] = right_ref[...]
    fill_outer(x_ref, left_ref[...], right_ref[...], high_ref, low_ref)
    split = first_ref.shape[0]
    end = x_ref.shape[1] - TILE
    first_ref[:, TILE:end] = inner_ref[:split, :]
    last_ref[:, TILE:end] = inner_ref[split:, :]
    for at, start in ((0, 0), (end, TILE + 2 * LANES)):
        value = filtered(high_ref, low_ref, band_ref, start)
        first_ref[:, at : at + TILE] = value[:split]
        last_ref[:, at : at + TILE] = value[split:]


def wall_sums(block_of, weight_ref, planes, store):
    rows = weight_ref.shape[0] // 2
    group = 6

    def some_planes(index, carry):
        for one in range(group):
            at = pl.ds(pl.multiple_of((index * group + one) * rows, rows), rows)
            high, low = block_of(at)
            both = dot(weight_ref[...], jnp.concatenate([high, low, high], axis=0))
            store(at, both[:rows], both[rows:])
        return carry

    lax.fori_loop(0, planes // group, some_planes, 0)


def own_sums_kernel(first_ref, last_ref, weight_ref, mine_ref, theirs_ref):
    rows = weight_ref.shape[0] // 2
    base = 0
    for own_ref in (first_ref, last_ref):

        def store(at, mine, theirs, base=base):
            to = pl.ds(pl.multiple_of(at.start + base, rows), rows)
            mine_ref[to, :] = mine
            theirs_ref[to, :] = theirs

        planes = own_ref.shape[0] // rows
        wall_sums(lambda at, own_ref=own_ref: halves(own_ref[at, :]), weight_ref, planes, store)
        base += own_ref.shape[0]


def far_sums_kernel(
    mine_own_ref, theirs_own_ref, far_ref, edge_ref, band_ref, weight_ref, mine_ref, theirs_ref,
    high_ref, low_ref, far_high_ref, far_low_ref,
):
    count = edge_ref.shape[0] // 2
    width = far_ref.shape[1]
    put(high_ref, low_ref, 0, spread(edge_ref[:count, :], True))
    put(high_ref, low_ref, LANES, far_ref[...])
    put(high_ref, low_ref, LANES + width, spread(edge_ref[count:, :], False))
    for at in range(0, width, TILE):
        put(far_high_ref, far_low_ref, at, filtered(high_ref, low_ref, band_ref, at))

    def store(at, mine, theirs):
        mine_ref[at, :] = mine_own_ref[at, :] + mine
        theirs_ref[at, :] = theirs_own_ref[at, :] + theirs

    planes = far_ref.shape[0] * 2 // weight_ref.shape[0]
    wall_sums(lambda at: (far_high_ref[at, :], far_low_ref[at, :]), weight_ref, planes, store)


def some_steps(
    base, mine_ref, theirs_ref, near_ref, weight_ref, row_ref, before_ref, velocity_ref,
    made_ref, field_ref, sems,
):
    rows = weight_ref.shape[0]
    repeat = near_ref.shape[1] // LANES

    def row(index):
        return jnp.concatenate([row_ref[index]] * repeat, axis=1)

    copies = []
    for step in range(near_ref.shape[0] // (3 * rows)):
        field = []
        for part in range(3):
            at = (step * 3 + part) * rows
            of = pl.ds(part * rows, rows)
            high, low = halves(near_ref[pl.ds(at, rows), :])
            total = mine_ref[pl.ds(base + at, rows), :] + theirs_ref[pl.ds(base + at, rows), :]
            total = total + dot(weight_ref[...], jnp.concatenate([high, low, high], axis=0))
            before = before_ref[of, :] if step == 0 else field_ref[of, :]
            now = row(part) * before + row(3 + part) * total
            field_ref[of, :] = now
            field.append(now)
        at = step * 3 * rows
        made_ref[pl.ds(at, rows), :] = row(12) + row(6) * field[0]
        made_ref[pl.ds(at + rows, rows), :] = row(7) * field[0] + row(8) * field[1]
        made_ref[pl.ds(at + 2 * rows, rows), :] = (
            row(9) * field[0] + row(10) * field[1] + row(11) * field[2]
        )
        copy = pltpu.make_async_copy(
            made_ref.at[pl.ds(at, 3 * rows)], velocity_ref.at[pl.ds(base + at, 3 * rows)],
            sems.at[step],
        )
        copy.start()
        copies.append(copy)
    return copies


def first_steps_kernel(
    mine_ref, theirs_ref, near_ref, weight_ref, row_ref, before_ref, velocity_ref, field_ref,
    made_ref, sems,
):
    for copy in some_steps(
        0, mine_ref, theirs_ref, near_ref, weight_ref, row_ref, before_ref, velocity_ref,
        made_ref, field_ref, sems,
    ):
        copy.wait()


def last_steps_kernel(
    _, mine_ref, theirs_ref, near_ref, weight_ref, row_ref, before_ref, velocity_ref, state_ref,
    made_ref, field_ref, sems,
):
    copies = some_steps(
        mine_ref.shape[0] - near_ref.shape[0], mine_ref, theirs_ref, near_ref, weight_ref,
        row_ref, before_ref, velocity_ref, made_ref, field_ref, sems,
    )
    copy = pltpu.make_async_copy(field_ref, state_ref, sems.at[len(copies)])
    copy.start()
    for one in copies + [copy]:
        one.wait()


WHOLE = pl.BlockSpec(memory_space=pltpu.VMEM)


def vmem(x):
    return pltpu.with_memory_space_constraint(x, pltpu.VMEM)


def hbm(x):
    return pltpu.with_memory_space_constraint(x, pltpu.HBM)


def call(kernel, out, scratch, flops, *args, in_specs=None, out_specs=None, **more):
    moved = sum(a.size * a.dtype.itemsize for a in args)
    return pl.pallas_call(
        kernel,
        out_shape=out,
        in_specs=in_specs or [WHOLE] * len(args),
        out_specs=out_specs or jax.tree.map(lambda _: WHOLE, out),
        scratch_shapes=scratch,
        cost_estimate=pl.CostEstimate(flops=flops, bytes_accessed=moved, transcendentals=0),
        compiler_params=pltpu.CompilerParams(vmem_limit_bytes=VMEM_BYTES),
        **more,
    )(*args)


def of_rows(scalars, rows):
    row = lax.broadcasted_iota(jnp.int32, (rows, LANES), 0)
    total = jnp.full((rows, LANES), scalars[0])
    for index in range(1, rows):
        total = jnp.where(row == index, scalars[index], total)
    return total


def weight_kernel(
    width_ref, other_ref, scale_ref, factor_ref, mean_ref, own_ref, far_ref, near_ref, row_ref
):
    rows = width_ref.shape[0]
    sign = 1 - 2 * (lax.axis_index("wall") % 2)
    lane = lax.broadcasted_iota(jnp.int32, (rows, LANES), 1)
    row = lax.broadcasted_iota(jnp.int32, (rows, LANES), 0)

    def raw(widths, offset):
        spread = widths.astype(f32)
        distance = offset.astype(f32)
        return jnp.where(
            jnp.abs(offset) <= widths,
            jnp.exp(-2.0 * math.pi * distance * distance / (spread * spread)),
            0.0,
        )

    def unit(widths, start):
        every = raw(widths, lane - HMAX)
        size = jnp.sqrt(jnp.sum(every * every, axis=1, keepdims=True))
        return raw(widths, lane % rows - row + start) / size

    def three(weights):
        high, low = halves(weights)
        return jnp.where(lane < 2 * rows, high.astype(f32), low.astype(f32))[:, : 3 * rows].astype(bf16)

    mine = of_rows([width_ref[i] for i in range(rows)], rows)
    other = of_rows([other_ref[i] for i in range(rows)], rows)
    own_ref[:rows, :] = three(unit(mine, 0))
    own_ref[rows:, :] = three(unit(other, -rows * sign))
    far_ref[:rows, :] = three(unit(mine, 2 * rows * sign))
    far_ref[rows:, :] = three(unit(other, rows * sign))
    near_ref[...] = three(unit(mine, -2 * rows * sign))
    for part in range(3):
        scale = of_rows([scale_ref[part, i] for i in range(rows)], rows)
        row_ref[part] = jnp.exp(-math.pi / (2.0 * scale))
        row_ref[3 + part] = jnp.sqrt(1.0 - jnp.exp(-math.pi / scale))
    for entry in range(6):
        row_ref[6 + entry] = of_rows([factor_ref[entry, i] for i in range(rows)], rows)
    row_ref[12] = of_rows([mean_ref[i] for i in range(rows)], rows)


def planes(random_planes, previous, half_width, time_scale, lund_factor, mean_velocity):
    steps, parts, rows, width = random_planes.shape
    wall = lax.axis_size("wall")
    span = lax.axis_size("span")
    near_pairs = []
    far_pairs = []
    for at in range(wall):
        way = 2 - 4 * (at % 2)
        if 0 <= at - way < wall:
            near_pairs.append((at - way, at))
        if 0 <= at + way < wall:
            far_pairs.append((at + way, at))
    swap = [(at, at ^ 1) for at in range(wall)]
    forward = [(i, (i + 1) % span) for i in range(span)]
    backward = [(target, source) for source, target in forward]

    x = random_planes.reshape(steps * parts * rows, width)
    count = x.shape[0]
    packed_rows = count * EDGE // LANES
    far = lax.ppermute(x, "wall", far_pairs)
    packed = pltpu.VMEM((packed_rows, LANES), f32)
    mine_right, mine_left = call(
        pack_kernel, (packed, packed), [], 0, hbm(x), hbm(x),
        in_specs=[
            pl.BlockSpec((count, LANES), lambda i: (0, 0)),
            pl.BlockSpec((count, LANES), lambda i: (0, width // LANES - 1)),
        ],
        grid=(1,),
    )
    left = lax.ppermute(mine_left, "span", forward)
    right = lax.ppermute(mine_right, "span", backward)

    band = jnp.asarray(span_band())
    split = max(steps - LAST_STEPS, 1) * parts * rows
    block = pltpu.VMEM(x.shape, f32)
    part = pltpu.VMEM((count, width - 2 * TILE), f32)
    inner = [pltpu.VMEM((count, width - 2 * TILE + 2 * LANES), bf16)] * 2
    outer = [pltpu.VMEM((count, 2 * TILE + 4 * LANES), bf16)] * 2
    window = [pltpu.VMEM((count, width + 2 * LANES), bf16)] * 2
    far_parts = [pltpu.VMEM((count, width), bf16)] * 2
    span_flops = count * width * 512 * 3
    wall_flops = count * width * 32 * 6
    own, band = call(
        own_inner_kernel, (part, pltpu.VMEM(band.shape, bf16)),
        inner + [pltpu.SemaphoreType.DMA(())], span_flops, vmem(x), hbm(band),
        in_specs=[WHOLE, pl.BlockSpec(memory_space=pl.ANY)],
    )
    own_first, own_last, far_edges = call(
        own_outer_kernel,
        (
            pltpu.VMEM((split, width), f32), pltpu.VMEM((count - split, width), f32),
            pltpu.VMEM((2 * packed_rows, LANES), f32),
        ),
        outer, span_flops, vmem(own), vmem(x), vmem(left), vmem(right), vmem(band),
    )
    near_first = lax.ppermute(own_first, "wall", near_pairs)
    near_last = lax.ppermute(own_last, "wall", near_pairs)
    far_edges = lax.ppermute(far_edges, "wall", far_pairs)
    other_width = lax.ppermute(half_width, "wall", swap)

    scalars = pl.BlockSpec(memory_space=pltpu.SMEM)
    own_both, far_both, near_w, per_row = call(
        weight_kernel,
        (
            pltpu.VMEM((2 * rows, 3 * rows), bf16), pltpu.VMEM((2 * rows, 3 * rows), bf16),
            pltpu.VMEM((rows, 3 * rows), bf16), pltpu.VMEM((13, rows, LANES), f32),
        ),
        [], 0, half_width, other_width, time_scale, lund_factor, mean_velocity,
        in_specs=[scalars] * 5,
    )
    mine, theirs = call(
        own_sums_kernel, (block, block), [], wall_flops, vmem(own_first),
        vmem(own_last), vmem(own_both),
    )
    mine, theirs = call(
        far_sums_kernel, (block, block), window + far_parts,
        2 * span_flops + wall_flops, vmem(mine), vmem(theirs), vmem(far), vmem(far_edges),
        vmem(band), vmem(far_both),
    )
    theirs = lax.ppermute(theirs, "wall", swap)
    mine, theirs, near_w, per_row = vmem(mine), vmem(theirs), vmem(near_w), vmem(per_row)
    line = (parts * rows, width)
    anywhere = pl.BlockSpec(memory_space=pl.ANY)
    velocity, field = call(
        first_steps_kernel,
        (jax.ShapeDtypeStruct(x.shape, f32), pltpu.VMEM(line, f32)),
        [pltpu.VMEM((split, width), f32), pltpu.SemaphoreType.DMA((steps,))],
        wall_flops, mine, theirs, vmem(near_first), near_w, per_row,
        vmem(previous.reshape(line)), out_specs=(anywhere, WHOLE),
    )
    velocity, state = call(
        last_steps_kernel,
        (jax.ShapeDtypeStruct(x.shape, f32), jax.ShapeDtypeStruct(line, f32)),
        [
            pltpu.VMEM((count - split, width), f32), pltpu.VMEM(line, f32),
            pltpu.SemaphoreType.DMA((steps + 1,)),
        ],
        wall_flops, velocity, mine, theirs, vmem(near_last), near_w, per_row, vmem(field),
        in_specs=[anywhere] + [WHOLE] * 6, out_specs=(anywhere, anywhere),
        input_output_aliases={0: 0},
    )
    return velocity.reshape(random_planes.shape), state.reshape(previous.shape)


def solution(mesh):
    in_specs = (
        P(None, None, "wall", "span"),
        P(None, "wall", "span"),
        P("wall"),
        P(None, "wall"),
        P(None, "wall"),
        P("wall"),
    )
    out_specs = (P(None, None, "wall", "span"), P(None, "wall", "span"))
    return jax.shard_map(planes, mesh=mesh, in_specs=in_specs, out_specs=out_specs, check_vma=False)
```

time: 52.7 us -> 58.7 us (1.11)
  the two profiles are of different devices: /device:TPU:262 before, /device:TPU:251 now
where the time goes in v2:
time: 58.7 us; the launch traced here: 58.3 us
  starting transfers between devices  25.5 us (43%)
  waiting for transfers between devices  21.3 us (36%)
  Pallas kernels  10.7 us (18%)
  between operations  0.83 us (1%)
    ppermute x1, waiting for transfers between devices, planes(): near_first = lax.ppermute(own_first, 'wall', near_pairs)  16.4 us
    pallas_call x8, Pallas kernels, call(): pl.pallas_call(kernel, out_shape=out, in_specs=in_specs or [WHOLE] * len(...  10.7 us
    ppermute x1, starting transfers between devices, planes(): theirs = lax.ppermute(theirs, 'wall', swap)  6.25 us
    ppermute x1, starting transfers between devices, planes(): far = lax.ppermute(x, 'wall', far_pairs)  4.55 us
    ppermute x1, starting transfers between devices, planes(): left = lax.ppermute(mine_left, 'span', forward)  3.12 us
    ppermute x1, starting transfers between devices, planes(): far_edges = lax.ppermute(far_edges, 'wall', far_pairs)  2.94 us
    ppermute x1, waiting for transfers between devices, planes(): near_last = lax.ppermute(own_last, 'wall', near_pairs)  2.8 us
    ppermute x1, starting transfers between devices, planes(): other_width = lax.ppermute(half_width, 'wall', swap)  2.61 us
  transfers between devices with their start and end apart: 8, of which 4 were waited for; matrix products, arithmetic and copies ran while one was open for 0% of the time, Pallas kernels for 12%

profile of v2, /device:TPU:251, one launch (start us, length us, event | category | flops | bytes accessed | tf_op | source)
XLA Modules:
  0.0 58.3 jit_solution(321320994141263937)
XLA Ops:
  0.6 0.0 copy-start
  0.6 4.5 %collective-permute-start.3 = (f32[384,1024]{1,0:T(8,128)}, f32[384,1024]{1,0:T(8,128)S(1)}, u32[]{:S(2)}, u32[]{:S(2)}) collective-permute-start(f32[384,1024]{1,0:T(8,128)} %bitcast.4), channel_id=1, source_target_pairs={{8,0},{16,8},{4,12},{24,16},{12,20},{32,24},{20,28},{40,32},{28,36... | collective-permute-start | bytes 4718600 | tf_op jit(solution)/shard_map/ppermute | solution.py:330
  5.2 1.2 %shard_map.87 = (f32[96,128]{1,0:T(8,128)S(1)}, f32[96,128]{1,0:T(8,128)S(1)}) custom-call(f32[384,1024]{1,0:T(8,128)} %bitcast.5, f32[384,1024]{1,0:T(8,128)} %bitcast.6), custom_call_target="tpu_custom_call" | custom-call | bytes 3145728 | tf_op jit(solution)/shard_map/pallas_call | solution.py:249
  6.4 3.1 %collective-permute-start = (f32[96,128]{1,0:T(8,128)S(1)}, f32[96,128]{1,0:T(8,128)S(1)}, u32[]{:S(2)}, u32[]{:S(2)}) collective-permute-start(f32[96,128]{1,0:T(8,128)S(1)} %get-tuple-element.22), channel_id=1, source_target_pairs={{0,1},{1,2},{2,3},{3,0},{4,5},{5,6},{6,7},{7,4},{8,9},{9,10},{10,1... | collective-permute-start | bytes 147464 | tf_op jit(solution)/shard_map/ppermute | solution.py:340
  9.5 2.2 %collective-permute-start.1 = (f32[96,128]{1,0:T(8,128)S(1)}, f32[96,128]{1,0:T(8,128)S(1)}, u32[]{:S(2)}, u32[]{:S(2)}) collective-permute-start(f32[96,128]{1,0:T(8,128)S(1)} %get-tuple-element.23), channel_id=1, source_target_pairs={{1,0},{2,1},{3,2},{0,3},{5,4},{6,5},{7,6},{4,7},{9,8},{10,9},{11,1... | collective-permute-start | bytes 147464 | tf_op jit(solution)/shard_map/ppermute | solution.py:341
  11.7 0.0 copy-done
  11.7 1.8 %shard_map.86 = (f32[384,512]{1,0:T(8,128)S(1)}, bf16[2,512,256]{2,1,0:T(8,128)(2,1)S(1)}) custom-call(f32[384,1024]{1,0:T(8,128)S(1)} %bitcast.7, bf16[2,512,256]{2,1,0:T(8,128)(2,1)} %constant.2.clone.band_hbm), custom_call_target="tpu_custom_call" | custom-call | flops 603979776 | bytes 2097152 | tf_op jit(solution)/shard_map/pallas_call | solution.py:249
  13.5 0.0 copy-start.4
  13.5 0.0 copy-start.2
  13.5 0.0 copy-start.3
  13.6 0.0 copy-start.5
  13.6 0.0 collective-permute-done.left_ref
  13.6 1.3 %collective-permute-done.1.right_ref = f32[96,128]{1,0:T(8,128)S(1)} collective-permute-done((f32[96,128]{1,0:T(8,128)S(1)}, f32[96,128]{1,0:T(8,128)S(1)}, u32[]{:S(2)}, u32[]{:S(2)}) %collective-permute-start.1) | collective-permute-done | bytes 49184 | tf_op jit(solution)/shard_map/ppermute | solution.py:341
  14.9 0.9 %shard_map.88 = (f32[288,1024]{1,0:T(8,128)S(1)}, f32[96,1024]{1,0:T(8,128)S(1)}, f32[192,128]{1,0:T(8,128)S(1)}) custom-call(f32[384,512]{1,0:T(8,128)S(1)} %get-tuple-element.21.inner_ref, f32[384,1024]{1,0:T(8,128)S(1)} %bitcast.8, f32[96,128]{1,0:T(8,128)S(1)} %collective-permute-done.left_ref, f32[96,128]{1,0:T(8,128)S(1)} %collective-permute-done.1.right_ref, ...), custom_call_target="tpu_custom_call" | custom-call | flops 603979776 | bytes 2981888 | tf_op jit(solution)/shard_map/pallas_call | solution.py:249
  15.8 2.9 %collective-permute-start.4 = (f32[192,128]{1,0:T(8,128)S(1)}, f32[192,128]{1,0:T(8,128)S(1)}, u32[]{:S(2)}, u32[]{:S(2)}) collective-permute-start(f32[192,128]{1,0:T(8,128)S(1)} %get-tuple-element.30), channel_id=1, source_target_pairs={{8,0},{16,8},{4,12},{24,16},{12,20},{32,24},{20,28},{40,32},{28,36... | collective-permute-start | bytes 294920 | tf_op jit(solution)/shard_map/ppermute | solution.py:368
  18.8 0.0 copy-done.4
  18.8 2.6 %collective-permute-start.2 = (s32[16]{0:T(128)S(1)}, s32[16]{0:T(128)S(1)}, u32[]{:S(2)}, u32[]{:S(2)}) collective-permute-start(s32[16]{0:T(128)S(1)} %copy-done.4), channel_id=1, source_target_pairs={{0,4},{4,0},{8,12},{12,8},{16,20},{20,16},{24,28},{28,24},{32,36},... | collective-permute-start | bytes 200 | tf_op jit(solution)/shard_map/ppermute | solution.py:369
  21.4 0.8 %collective-permute-done.2.other_ref = s32[16]{0:T(128)S(1)} collective-permute-done((s32[16]{0:T(128)S(1)}, s32[16]{0:T(128)S(1)}, u32[]{:S(2)}, u32[]{:S(2)}) %collective-permute-start.2) | collective-permute-done | bytes 96 | tf_op jit(solution)/shard_map/ppermute | solution.py:369
  22.2 0.0 copy-done.2
  22.2 0.0 copy-done.3
  22.2 0.0 copy-done.5
  22.2 0.8 %shard_map.89 = (bf16[32,48]{1,0:T(8,128)(2,1)S(1)}, bf16[32,48]{1,0:T(8,128)(2,1)S(1)}, bf16[16,48]{1,0:T(8,128)(2,1)S(1)}, f32[13,16,128]{2,1,0:T(8,128)S(1)}) custom-call(s32[16]{0:T(128)S(1)} %copy-done.4, s32[16]{0:T(128)S(1)} %collective-permute-done.2.other_ref, f32[3,16]{1,0:T(4,128)S(1)} %copy-done.3, f32[6,16]{1,0:T(8,128)S(1)} %copy-done.2, ...), custom_call_target="tpu_custom_call" | custom-call | bytes 768 | tf_op jit(solution)/shard_map/pallas_call | solution.py:249
  23.0 1.0 %shard_map.90 = (f32[384,1024]{1,0:T(8,128)S(1)}, f32[384,1024]{1,0:T(8,128)S(1)}) custom-call(f32[288,1024]{1,0:T(8,128)S(1)} %get-tuple-element.25.first_ref, f32[96,1024]{1,0:T(8,128)S(1)} %get-tuple-element.26.last_ref, bf16[32,48]{1,0:T(8,128)(2,1)S(1)} %get-tuple-element.27.weight_ref), custom_call_target="tpu_custom_call" | custom-call | flops 75497472 | bytes 1575936 | tf_op jit(solution)/shard_map/pallas_call | solution.py:249
  24.0 0.0 collective-permute-done.4.edge_ref
  24.0 0.0 collective-permute-done.3.far_ref
  24.0 0.0 copy-start.1
  24.0 2.5 %shard_map.91 = (f32[384,1024]{1,0:T(8,128)S(1)}, f32[384,1024]{1,0:T(8,128)S(1)}) custom-call(f32[384,1024]{1,0:T(8,128)S(1)} %get-tuple-element.28.mine_own_ref, f32[384,1024]{1,0:T(8,128)S(1)} %get-tuple-element.29.theirs_own_ref, f32[384,1024]{1,0:T(8,128)S(1)} %collective-permute-done.3.far_ref, f32[192,128]{1,0:T(8,128)S(1)} %collective-permute-done.4.edge_ref, ...), custom_call_target="tpu_custom_call" | custom-call | flops 1283457024 | bytes 5344256 | tf_op jit(solution)/shard_map/pallas_call | solution.py:249
  26.5 6.3 %collective-permute-start.5 = (f32[384,1024]{1,0:T(8,128)S(1)}, f32[384,1024]{1,0:T(8,128)S(1)}, u32[]{:S(2)}, u32[]{:S(2)}) collective-permute-start(f32[384,1024]{1,0:T(8,128)S(1)} %get-tuple-element.33), channel_id=1, source_target_pairs={{0,4},{4,0},{8,12},{12,8},{16,20},{20,16},{24,28},{28,24},{32,36},... | collective-permute-start | bytes 4718600 | tf_op jit(solution)/shard_map/ppermute | solution.py:390
  32.8 1.9 %collective-permute-start.6 = (f32[288,1024]{1,0:T(8,128)S(1)}, f32[288,1024]{1,0:T(8,128)S(1)}, u32[]{:S(2)}, u32[]{:S(2)}) collective-permute-start(f32[288,1024]{1,0:T(8,128)S(1)} %get-tuple-element.25.first_ref), channel_id=1, source_target_pairs={{12,4},{0,8},{20,12},{8,16},{28,20},{16,24},{36,28},{24,32},{44,36... | collective-permute-start | bytes 3538952 | tf_op jit(solution)/shard_map/ppermute | solution.py:366
  34.7 1.9 %collective-permute-start.7 = (f32[96,1024]{1,0:T(8,128)S(1)}, f32[96,1024]{1,0:T(8,128)S(1)}, u32[]{:S(2)}, u32[]{:S(2)}) collective-permute-start(f32[96,1024]{1,0:T(8,128)S(1)} %get-tuple-element.26.last_ref), channel_id=1, source_target_pairs={{12,4},{0,8},{20,12},{8,16},{28,20},{16,24},{36,28},{24,32},{44,36... | collective-permute-start | bytes 1179656 | tf_op jit(solution)/shard_map/ppermute | solution.py:367
  36.6 16.4 %collective-permute-done.6.near_ref = f32[288,1024]{1,0:T(8,128)S(1)} collective-permute-done((f32[288,1024]{1,0:T(8,128)S(1)}, f32[288,1024]{1,0:T(8,128)S(1)}, u32[]{:S(2)}, u32[]{:S(2)}) %collective-permute-start.6) | collective-permute-done | bytes 1179680 | tf_op jit(solution)/shard_map/ppermute | solution.py:366
  53.1 0.0 collective-permute-done.5.theirs_ref
  53.1 0.0 copy-done.1
  53.1 1.4 %shard_map.92 = (f32[384,1024]{1,0:T(8,128)}, f32[48,1024]{1,0:T(8,128)S(1)}) custom-call(f32[384,1024]{1,0:T(8,128)S(1)} %get-tuple-element.32.mine_ref, f32[384,1024]{1,0:T(8,128)S(1)} %collective-permute-done.5.theirs_ref, f32[288,1024]{1,0:T(8,128)S(1)} %collective-permute-done.6.near_ref, bf16[16,48]{1,0:T(8,128)(2,1)S(1)} %get-tuple-element.34.weight_ref, ...), custom_call_target="tpu_custom_call" | custom-call | flops 75497472 | bytes 4630016 | tf_op jit(solution)/shard_map/pallas_call | solution.py:249
  54.5 2.8 %collective-permute-done.7.near_ref = f32[96,1024]{1,0:T(8,128)S(1)} collective-permute-done((f32[96,1024]{1,0:T(8,128)S(1)}, f32[96,1024]{1,0:T(8,128)S(1)}, u32[]{:S(2)}, u32[]{:S(2)}) %collective-permute-start.7) | collective-permute-done | bytes 393248 | tf_op jit(solution)/shard_map/ppermute | solution.py:367
  57.3 1.1 %shard_map.93 = (f32[384,1024]{1,0:T(8,128)}, f32[48,1024]{1,0:T(8,128)}) custom-call(f32[384,1024]{1,0:T(8,128)} %get-tuple-element.36._, f32[384,1024]{1,0:T(8,128)S(1)} %get-tuple-element.32.mine_ref, f32[384,1024]{1,0:T(8,128)S(1)} %collective-permute-done.5.theirs_ref, ...), custom_call_target="tpu_custom_call", output_to_operand_aliasing={{0}: (0, {})} | custom-call | flops 75497472 | bytes 5416448 | tf_op jit(solution)/shard_map/pallas_call | solution.py:249
Async XLA Ops:
  0.6 11.0 %copy-start = (f32[8,3,16,1024]{3,2,1,0:T(8,128)S(1)}, f32[8,3,16,1024]{3,2,1,0:T(8,128)}, u32[]{:S(2)}) copy-start(f32[8,3,16,1024]{3,2,1,0:T(8,128)} %param.7) | copy-start | bytes 4718596
  0.6 23.4 %collective-permute-start.3 = (f32[384,1024]{1,0:T(8,128)}, f32[384,1024]{1,0:T(8,128)S(1)}, u32[]{:S(2)}, u32[]{:S(2)}) collective-permute-start(f32[384,1024]{1,0:T(8,128)} %bitcast.4), channel_id=1, source_target_pairs={{8,0},{16,8},{4,12},{24,16},{12,20},{32,24},{20,28},{40,32},{28,36... | collective-permute-start | bytes 4718600 | tf_op jit(solution)/shard_map/ppermute | solution.py:330
  6.4 7.2 %collective-permute-start = (f32[96,128]{1,0:T(8,128)S(1)}, f32[96,128]{1,0:T(8,128)S(1)}, u32[]{:S(2)}, u32[]{:S(2)}) collective-permute-start(f32[96,128]{1,0:T(8,128)S(1)} %get-tuple-element.22), channel_id=1, source_target_pairs={{0,1},{1,2},{2,3},{3,0},{4,5},{5,6},{6,7},{7,4},{8,9},{9,10},{10,1... | collective-permute-start | bytes 147464 | tf_op jit(solution)/shard_map/ppermute | solution.py:340
  9.5 5.4 %collective-permute-start.1 = (f32[96,128]{1,0:T(8,128)S(1)}, f32[96,128]{1,0:T(8,128)S(1)}, u32[]{:S(2)}, u32[]{:S(2)}) collective-permute-start(f32[96,128]{1,0:T(8,128)S(1)} %get-tuple-element.23), channel_id=1, source_target_pairs={{1,0},{2,1},{3,2},{0,3},{5,4},{6,5},{7,6},{4,7},{9,8},{10,9},{11,1... | collective-permute-start | bytes 147464 | tf_op jit(solution)/shard_map/ppermute | solution.py:341
  13.5 5.3 %copy-start.4 = (s32[16]{0:T(128)S(1)}, s32[16]{0:T(128)}, u32[]{:S(2)}) copy-start(s32[16]{0:T(128)} %width_ref.1) | copy-start | bytes 196
  13.5 8.7 %copy-start.2 = (f32[6,16]{1,0:T(8,128)S(1)}, f32[6,16]{1,0:T(8,128)}, u32[]{:S(2)}) copy-start(f32[6,16]{1,0:T(8,128)} %factor_ref.1) | copy-start | bytes 1156
  13.5 8.7 %copy-start.3 = (f32[3,16]{1,0:T(4,128)S(1)}, f32[3,16]{1,0:T(4,128)}, u32[]{:S(2)}) copy-start(f32[3,16]{1,0:T(4,128)} %scale_ref.1) | copy-start | bytes 580
  13.6 8.7 %copy-start.5 = (f32[16]{0:T(128)S(1)}, f32[16]{0:T(128)}, u32[]{:S(2)}) copy-start(f32[16]{0:T(128)} %mean_ref.1) | copy-start | bytes 196
  15.8 8.2 %collective-permute-start.4 = (f32[192,128]{1,0:T(8,128)S(1)}, f32[192,128]{1,0:T(8,128)S(1)}, u32[]{:S(2)}, u32[]{:S(2)}) collective-permute-start(f32[192,128]{1,0:T(8,128)S(1)} %get-tuple-element.30), channel_id=1, source_target_pairs={{8,0},{16,8},{4,12},{24,16},{12,20},{32,24},{20,28},{40,32},{28,36... | collective-permute-start | bytes 294920 | tf_op jit(solution)/shard_map/ppermute | solution.py:368
  18.8 3.4 %collective-permute-start.2 = (s32[16]{0:T(128)S(1)}, s32[16]{0:T(128)S(1)}, u32[]{:S(2)}, u32[]{:S(2)}) collective-permute-start(s32[16]{0:T(128)S(1)} %copy-done.4), channel_id=1, source_target_pairs={{0,4},{4,0},{8,12},{12,8},{16,20},{20,16},{24,28},{28,24},{32,36},... | collective-permute-start | bytes 200 | tf_op jit(solution)/shard_map/ppermute | solution.py:369
  24.0 29.1 %copy-start.1 = (f32[3,16,1024]{2,1,0:T(8,128)S(1)}, f32[3,16,1024]{2,1,0:T(8,128)}, u32[]{:S(2)}) copy-start(f32[3,16,1024]{2,1,0:T(8,128)} %param.8) | copy-start | bytes 589828
  26.5 26.5 %collective-permute-start.5 = (f32[384,1024]{1,0:T(8,128)S(1)}, f32[384,1024]{1,0:T(8,128)S(1)}, u32[]{:S(2)}, u32[]{:S(2)}) collective-permute-start(f32[384,1024]{1,0:T(8,128)S(1)} %get-tuple-element.33), channel_id=1, source_target_pairs={{0,4},{4,0},{8,12},{12,8},{16,20},{20,16},{24,28},{28,24},{32,36},... | collective-permute-start | bytes 4718600 | tf_op jit(solution)/shard_map/ppermute | solution.py:390
  32.8 20.3 %collective-permute-start.6 = (f32[288,1024]{1,0:T(8,128)S(1)}, f32[288,1024]{1,0:T(8,128)S(1)}, u32[]{:S(2)}, u32[]{:S(2)}) collective-permute-start(f32[288,1024]{1,0:T(8,128)S(1)} %get-tuple-element.25.first_ref), channel_id=1, source_target_pairs={{12,4},{0,8},{20,12},{8,16},{28,20},{16,24},{36,28},{24,32},{44,36... | collective-permute-start | bytes 3538952 | tf_op jit(solution)/shard_map/ppermute | solution.py:366
  34.7 22.6 %collective-permute-start.7 = (f32[96,1024]{1,0:T(8,128)S(1)}, f32[96,1024]{1,0:T(8,128)S(1)}, u32[]{:S(2)}, u32[]{:S(2)}) collective-permute-start(f32[96,1024]{1,0:T(8,128)S(1)} %get-tuple-element.26.last_ref), channel_id=1, source_target_pairs={{12,4},{0,8},{20,12},{8,16},{28,20},{16,24},{36,28},{24,32},{44,36... | collective-permute-start | bytes 1179656 | tf_op jit(solution)/shard_map/ppermute | solution.py:367

commit v3 on v2

--- a/solution.py
+++ b/solution.py
@@ -296,8 +296,8 @@
     other = of_rows([other_ref[i] for i in range(rows)], rows)
     own_ref[:rows, :] = three(unit(mine, 0))
     own_ref[rows:, :] = three(unit(other, -rows * sign))
-    far_ref[:rows, :] = three(unit(mine, 2 * rows * sign))
-    far_ref[rows:, :] = three(unit(other, rows * sign))
+    far_ref[:rows, :] = three(unit(mine, -rows * sign))
+    far_ref[rows:, :] = three(unit(other, -2 * rows * sign))
     near_ref[...] = three(unit(mine, -2 * rows * sign))
     for part in range(3):
         scale = of_rows([scale_ref[part, i] for i in range(rows)], rows)
@@ -315,11 +315,11 @@
     near_pairs = []
     far_pairs = []
     for at in range(wall):
-        way = 2 - 4 * (at % 2)
-        if 0 <= at - way < wall:
-            near_pairs.append((at - way, at))
-        if 0 <= at + way < wall:
-            far_pairs.append((at + way, at))
+        step = 1 - 2 * (at % 2)
+        if 0 <= at - step < wall:
+            far_pairs.append((at - step, at))
+        if 0 <= at - 2 * step < wall:
+            near_pairs.append((at - 2 * step, at))
     swap = [(at, at ^ 1) for at in range(wall)]
     forward = [(i, (i + 1) % span) for i in range(span)]
     backward = [(target, source) for source, target in forward]

time: 58.7 us -> 58.6 us (level)
  the two profiles are of different devices: /device:TPU:251 before, /device:TPU:262 now
where the time goes in v3:
time: 58.6 us; the launch traced here: 58.3 us
  waiting for transfers between devices  25.6 us (44%)
  starting transfers between devices  21.1 us (36%)
  Pallas kernels  10.7 us (18%)
  between operations  0.81 us (1%)
    ppermute x1, waiting for transfers between devices, planes(): near_first = lax.ppermute(own_first, 'wall', near_pairs)  17.6 us
    pallas_call x8, Pallas kernels, call(): pl.pallas_call(kernel, out_shape=out, in_specs=in_specs or [WHOLE] * len(...  10.7 us
    ppermute x1, starting transfers between devices, planes(): far = lax.ppermute(x, 'wall', far_pairs)  4.04 us
    ppermute x1, starting transfers between devices, planes(): far_edges = lax.ppermute(far_edges, 'wall', far_pairs)  3.55 us
    ppermute x1, starting transfers between devices, planes(): right = lax.ppermute(mine_right, 'span', backward)  3.46 us
    ppermute x1, waiting for transfers between devices, planes(): near_last = lax.ppermute(own_last, 'wall', near_pairs)  2.8 us
    ppermute x1, starting transfers between devices, planes(): left = lax.ppermute(mine_left, 'span', forward)  2.39 us
    ppermute x1, waiting for transfers between devices, planes(): far_edges = lax.ppermute(far_edges, 'wall', far_pairs)  2.29 us
  transfers between devices with their start and end apart: 8, of which 5 were waited for; matrix products, arithmetic and copies ran while one was open for 0% of the time, Pallas kernels for 12%

profile of v3, /device:TPU:262, one launch (start us, length us, event | category | flops | bytes accessed | tf_op | source)
XLA Modules:
  0.0 58.3 jit_solution(964042695618609152)
XLA Ops:
  0.6 0.0 copy-start
  0.6 4.0 %collective-permute-start.3 = (f32[384,1024]{1,0:T(8,128)}, f32[384,1024]{1,0:T(8,128)S(1)}, u32[]{:S(2)}, u32[]{:S(2)}) collective-permute-start(f32[384,1024]{1,0:T(8,128)} %bitcast.4), channel_id=1, source_target_pairs={{8,4},{4,8},{16,12},{12,16},{24,20},{20,24},{32,28},{28,32},{40,36... | collective-permute-start | bytes 4718600 | tf_op jit(solution)/shard_map/ppermute | solution.py:330
  4.7 1.2 %shard_map.87 = (f32[96,128]{1,0:T(8,128)S(1)}, f32[96,128]{1,0:T(8,128)S(1)}) custom-call(f32[384,1024]{1,0:T(8,128)} %bitcast.5, f32[384,1024]{1,0:T(8,128)} %bitcast.6), custom_call_target="tpu_custom_call" | custom-call | bytes 3145728 | tf_op jit(solution)/shard_map/pallas_call | solution.py:249
  5.9 2.4 %collective-permute-start = (f32[96,128]{1,0:T(8,128)S(1)}, f32[96,128]{1,0:T(8,128)S(1)}, u32[]{:S(2)}, u32[]{:S(2)}) collective-permute-start(f32[96,128]{1,0:T(8,128)S(1)} %get-tuple-element.22), channel_id=1, source_target_pairs={{0,1},{1,2},{2,3},{3,0},{4,5},{5,6},{6,7},{7,4},{8,9},{9,10},{10,1... | collective-permute-start | bytes 147464 | tf_op jit(solution)/shard_map/ppermute | solution.py:340
  8.3 3.5 %collective-permute-start.1 = (f32[96,128]{1,0:T(8,128)S(1)}, f32[96,128]{1,0:T(8,128)S(1)}, u32[]{:S(2)}, u32[]{:S(2)}) collective-permute-start(f32[96,128]{1,0:T(8,128)S(1)} %get-tuple-element.23), channel_id=1, source_target_pairs={{1,0},{2,1},{3,2},{0,3},{5,4},{6,5},{7,6},{4,7},{9,8},{10,9},{11,1... | collective-permute-start | bytes 147464 | tf_op jit(solution)/shard_map/ppermute | solution.py:341
  11.7 0.0 copy-done
  11.7 1.8 %shard_map.86 = (f32[384,512]{1,0:T(8,128)S(1)}, bf16[2,512,256]{2,1,0:T(8,128)(2,1)S(1)}) custom-call(f32[384,1024]{1,0:T(8,128)S(1)} %bitcast.7, bf16[2,512,256]{2,1,0:T(8,128)(2,1)} %constant.2.clone.band_hbm), custom_call_target="tpu_custom_call" | custom-call | flops 603979776 | bytes 2097152 | tf_op jit(solution)/shard_map/pallas_call | solution.py:249
  13.6 0.0 copy-start.4
  13.6 0.0 copy-start.2
  13.6 0.0 copy-start.3
  13.6 0.0 copy-start.5
  13.6 0.0 collective-permute-done.left_ref
  13.6 1.8 %collective-permute-done.1.right_ref = f32[96,128]{1,0:T(8,128)S(1)} collective-permute-done((f32[96,128]{1,0:T(8,128)S(1)}, f32[96,128]{1,0:T(8,128)S(1)}, u32[]{:S(2)}, u32[]{:S(2)}) %collective-permute-start.1) | collective-permute-done | bytes 49184 | tf_op jit(solution)/shard_map/ppermute | solution.py:341
  15.4 0.9 %shard_map.88 = (f32[288,1024]{1,0:T(8,128)S(1)}, f32[96,1024]{1,0:T(8,128)S(1)}, f32[192,128]{1,0:T(8,128)S(1)}) custom-call(f32[384,512]{1,0:T(8,128)S(1)} %get-tuple-element.21.inner_ref, f32[384,1024]{1,0:T(8,128)S(1)} %bitcast.8, f32[96,128]{1,0:T(8,128)S(1)} %collective-permute-done.left_ref, f32[96,128]{1,0:T(8,128)S(1)} %collective-permute-done.1.right_ref, ...), custom_call_target="tpu_custom_call" | custom-call | flops 603979776 | bytes 2981888 | tf_op jit(solution)/shard_map/pallas_call | solution.py:249
  16.4 3.5 %collective-permute-start.4 = (f32[192,128]{1,0:T(8,128)S(1)}, f32[192,128]{1,0:T(8,128)S(1)}, u32[]{:S(2)}, u32[]{:S(2)}) collective-permute-start(f32[192,128]{1,0:T(8,128)S(1)} %get-tuple-element.30), channel_id=1, source_target_pairs={{8,4},{4,8},{16,12},{12,16},{24,20},{20,24},{32,28},{28,32},{40,36... | collective-permute-start | bytes 294920 | tf_op jit(solution)/shard_map/ppermute | solution.py:368
  19.9 0.0 copy-done.4
  19.9 1.9 %collective-permute-start.2 = (s32[16]{0:T(128)S(1)}, s32[16]{0:T(128)S(1)}, u32[]{:S(2)}, u32[]{:S(2)}) collective-permute-start(s32[16]{0:T(128)S(1)} %copy-done.4), channel_id=1, source_target_pairs={{0,4},{4,0},{8,12},{12,8},{16,20},{20,16},{24,28},{28,24},{32,36},... | collective-permute-start | bytes 200 | tf_op jit(solution)/shard_map/ppermute | solution.py:369
  21.9 1.1 %collective-permute-done.2.other_ref = s32[16]{0:T(128)S(1)} collective-permute-done((s32[16]{0:T(128)S(1)}, s32[16]{0:T(128)S(1)}, u32[]{:S(2)}, u32[]{:S(2)}) %collective-permute-start.2) | collective-permute-done | bytes 96 | tf_op jit(solution)/shard_map/ppermute | solution.py:369
  23.0 0.0 copy-done.2
  23.0 0.0 copy-done.3
  23.0 0.0 copy-done.5
  23.0 0.8 %shard_map.89 = (bf16[32,48]{1,0:T(8,128)(2,1)S(1)}, bf16[32,48]{1,0:T(8,128)(2,1)S(1)}, bf16[16,48]{1,0:T(8,128)(2,1)S(1)}, f32[13,16,128]{2,1,0:T(8,128)S(1)}) custom-call(s32[16]{0:T(128)S(1)} %copy-done.4, s32[16]{0:T(128)S(1)} %collective-permute-done.2.other_ref, f32[3,16]{1,0:T(4,128)S(1)} %copy-done.3, f32[6,16]{1,0:T(8,128)S(1)} %copy-done.2, ...), custom_call_target="tpu_custom_call" | custom-call | bytes 768 | tf_op jit(solution)/shard_map/pallas_call | solution.py:249
  23.8 1.0 %shard_map.90 = (f32[384,1024]{1,0:T(8,128)S(1)}, f32[384,1024]{1,0:T(8,128)S(1)}) custom-call(f32[288,1024]{1,0:T(8,128)S(1)} %get-tuple-element.25.first_ref, f32[96,1024]{1,0:T(8,128)S(1)} %get-tuple-element.26.last_ref, bf16[32,48]{1,0:T(8,128)(2,1)S(1)} %get-tuple-element.27.weight_ref), custom_call_target="tpu_custom_call" | custom-call | flops 75497472 | bytes 1575936 | tf_op jit(solution)/shard_map/pallas_call | solution.py:249
  24.8 2.3 %collective-permute-done.4.edge_ref = f32[192,128]{1,0:T(8,128)S(1)} collective-permute-done((f32[192,128]{1,0:T(8,128)S(1)}, f32[192,128]{1,0:T(8,128)S(1)}, u32[]{:S(2)}, u32[]{:S(2)}) %collective-permute-start.4) | collective-permute-done | bytes 98336 | tf_op jit(solution)/shard_map/ppermute | solution.py:368
  27.1 0.0 collective-permute-done.3.far_ref
  27.1 0.0 copy-start.1
  27.1 2.5 %shard_map.91 = (f32[384,1024]{1,0:T(8,128)S(1)}, f32[384,1024]{1,0:T(8,128)S(1)}) custom-call(f32[384,1024]{1,0:T(8,128)S(1)} %get-tuple-element.28.mine_own_ref, f32[384,1024]{1,0:T(8,128)S(1)} %get-tuple-element.29.theirs_own_ref, f32[384,1024]{1,0:T(8,128)S(1)} %collective-permute-done.3.far_ref, f32[192,128]{1,0:T(8,128)S(1)} %collective-permute-done.4.edge_ref, ...), custom_call_target="tpu_custom_call" | custom-call | flops 1283457024 | bytes 5344256 | tf_op jit(solution)/shard_map/pallas_call | solution.py:249
  29.6 1.9 %collective-permute-start.5 = (f32[384,1024]{1,0:T(8,128)S(1)}, f32[384,1024]{1,0:T(8,128)S(1)}, u32[]{:S(2)}, u32[]{:S(2)}) collective-permute-start(f32[384,1024]{1,0:T(8,128)S(1)} %get-tuple-element.33), channel_id=1, source_target_pairs={{0,4},{4,0},{8,12},{12,8},{16,20},{20,16},{24,28},{28,24},{32,36},... | collective-permute-start | bytes 4718600 | tf_op jit(solution)/shard_map/ppermute | solution.py:390
  31.6 1.9 %collective-permute-start.6 = (f32[288,1024]{1,0:T(8,128)S(1)}, f32[288,1024]{1,0:T(8,128)S(1)}, u32[]{:S(2)}, u32[]{:S(2)}) collective-permute-start(f32[288,1024]{1,0:T(8,128)S(1)} %get-tuple-element.25.first_ref), channel_id=1, source_target_pairs={{12,4},{0,8},{20,12},{8,16},{28,20},{16,24},{36,28},{24,32},{44,36... | collective-permute-start | bytes 3538952 | tf_op jit(solution)/shard_map/ppermute | solution.py:366
  33.5 1.9 %collective-permute-start.7 = (f32[96,1024]{1,0:T(8,128)S(1)}, f32[96,1024]{1,0:T(8,128)S(1)}, u32[]{:S(2)}, u32[]{:S(2)}) collective-permute-start(f32[96,1024]{1,0:T(8,128)S(1)} %get-tuple-element.26.last_ref), channel_id=1, source_target_pairs={{12,4},{0,8},{20,12},{8,16},{28,20},{16,24},{36,28},{24,32},{44,36... | collective-permute-start | bytes 1179656 | tf_op jit(solution)/shard_map/ppermute | solution.py:367
  35.4 17.6 %collective-permute-done.6.near_ref = f32[288,1024]{1,0:T(8,128)S(1)} collective-permute-done((f32[288,1024]{1,0:T(8,128)S(1)}, f32[288,1024]{1,0:T(8,128)S(1)}, u32[]{:S(2)}, u32[]{:S(2)}) %collective-permute-start.6) | collective-permute-done | bytes 1179680 | tf_op jit(solution)/shard_map/ppermute | solution.py:366
  53.0 0.0 collective-permute-done.5.theirs_ref
  53.0 0.0 copy-done.1
  53.0 1.4 %shard_map.92 = (f32[384,1024]{1,0:T(8,128)}, f32[48,1024]{1,0:T(8,128)S(1)}) custom-call(f32[384,1024]{1,0:T(8,128)S(1)} %get-tuple-element.32.mine_ref, f32[384,1024]{1,0:T(8,128)S(1)} %collective-permute-done.5.theirs_ref, f32[288,1024]{1,0:T(8,128)S(1)} %collective-permute-done.6.near_ref, bf16[16,48]{1,0:T(8,128)(2,1)S(1)} %get-tuple-element.34.weight_ref, ...), custom_call_target="tpu_custom_call" | custom-call | flops 75497472 | bytes 4630016 | tf_op jit(solution)/shard_map/pallas_call | solution.py:249
  54.4 2.8 %collective-permute-done.7.near_ref = f32[96,1024]{1,0:T(8,128)S(1)} collective-permute-done((f32[96,1024]{1,0:T(8,128)S(1)}, f32[96,1024]{1,0:T(8,128)S(1)}, u32[]{:S(2)}, u32[]{:S(2)}) %collective-permute-start.7) | collective-permute-done | bytes 393248 | tf_op jit(solution)/shard_map/ppermute | solution.py:367
  57.2 1.1 %shard_map.93 = (f32[384,1024]{1,0:T(8,128)}, f32[48,1024]{1,0:T(8,128)}) custom-call(f32[384,1024]{1,0:T(8,128)} %get-tuple-element.36._, f32[384,1024]{1,0:T(8,128)S(1)} %get-tuple-element.32.mine_ref, f32[384,1024]{1,0:T(8,128)S(1)} %collective-permute-done.5.theirs_ref, ...), custom_call_target="tpu_custom_call", output_to_operand_aliasing={{0}: (0, {})} | custom-call | flops 75497472 | bytes 5416448 | tf_op jit(solution)/shard_map/pallas_call | solution.py:249
Async XLA Ops:
  0.6 11.1 %copy-start = (f32[8,3,16,1024]{3,2,1,0:T(8,128)S(1)}, f32[8,3,16,1024]{3,2,1,0:T(8,128)}, u32[]{:S(2)}) copy-start(f32[8,3,16,1024]{3,2,1,0:T(8,128)} %param.7) | copy-start | bytes 4718596
  0.6 26.5 %collective-permute-start.3 = (f32[384,1024]{1,0:T(8,128)}, f32[384,1024]{1,0:T(8,128)S(1)}, u32[]{:S(2)}, u32[]{:S(2)}) collective-permute-start(f32[384,1024]{1,0:T(8,128)} %bitcast.4), channel_id=1, source_target_pairs={{8,4},{4,8},{16,12},{12,16},{24,20},{20,24},{32,28},{28,32},{40,36... | collective-permute-start | bytes 4718600 | tf_op jit(solution)/shard_map/ppermute | solution.py:330
  5.9 7.8 %collective-permute-start = (f32[96,128]{1,0:T(8,128)S(1)}, f32[96,128]{1,0:T(8,128)S(1)}, u32[]{:S(2)}, u32[]{:S(2)}) collective-permute-start(f32[96,128]{1,0:T(8,128)S(1)} %get-tuple-element.22), channel_id=1, source_target_pairs={{0,1},{1,2},{2,3},{3,0},{4,5},{5,6},{6,7},{7,4},{8,9},{9,10},{10,1... | collective-permute-start | bytes 147464 | tf_op jit(solution)/shard_map/ppermute | solution.py:340
  8.3 7.2 %collective-permute-start.1 = (f32[96,128]{1,0:T(8,128)S(1)}, f32[96,128]{1,0:T(8,128)S(1)}, u32[]{:S(2)}, u32[]{:S(2)}) collective-permute-start(f32[96,128]{1,0:T(8,128)S(1)} %get-tuple-element.23), channel_id=1, source_target_pairs={{1,0},{2,1},{3,2},{0,3},{5,4},{6,5},{7,6},{4,7},{9,8},{10,9},{11,1... | collective-permute-start | bytes 147464 | tf_op jit(solution)/shard_map/ppermute | solution.py:341
  13.6 6.4 %copy-start.4 = (s32[16]{0:T(128)S(1)}, s32[16]{0:T(128)}, u32[]{:S(2)}) copy-start(s32[16]{0:T(128)} %width_ref.1) | copy-start | bytes 196
  13.6 9.4 %copy-start.2 = (f32[6,16]{1,0:T(8,128)S(1)}, f32[6,16]{1,0:T(8,128)}, u32[]{:S(2)}) copy-start(f32[6,16]{1,0:T(8,128)} %factor_ref.1) | copy-start | bytes 1156
  13.6 9.4 %copy-start.3 = (f32[3,16]{1,0:T(4,128)S(1)}, f32[3,16]{1,0:T(4,128)}, u32[]{:S(2)}) copy-start(f32[3,16]{1,0:T(4,128)} %scale_ref.1) | copy-start | bytes 580
  13.6 9.4 %copy-start.5 = (f32[16]{0:T(128)S(1)}, f32[16]{0:T(128)}, u32[]{:S(2)}) copy-start(f32[16]{0:T(128)} %mean_ref.1) | copy-start | bytes 196
  16.4 10.7 %collective-permute-start.4 = (f32[192,128]{1,0:T(8,128)S(1)}, f32[192,128]{1,0:T(8,128)S(1)}, u32[]{:S(2)}, u32[]{:S(2)}) collective-permute-start(f32[192,128]{1,0:T(8,128)S(1)} %get-tuple-element.30), channel_id=1, source_target_pairs={{8,4},{4,8},{16,12},{12,16},{24,20},{20,24},{32,28},{28,32},{40,36... | collective-permute-start | bytes 294920 | tf_op jit(solution)/shard_map/ppermute | solution.py:368
  19.9 3.1 %collective-permute-start.2 = (s32[16]{0:T(128)S(1)}, s32[16]{0:T(128)S(1)}, u32[]{:S(2)}, u32[]{:S(2)}) collective-permute-start(s32[16]{0:T(128)S(1)} %copy-done.4), channel_id=1, source_target_pairs={{0,4},{4,0},{8,12},{12,8},{16,20},{20,16},{24,28},{28,24},{32,36},... | collective-permute-start | bytes 200 | tf_op jit(solution)/shard_map/ppermute | solution.py:369
  27.1 25.9 %copy-start.1 = (f32[3,16,1024]{2,1,0:T(8,128)S(1)}, f32[3,16,1024]{2,1,0:T(8,128)}, u32[]{:S(2)}) copy-start(f32[3,16,1024]{2,1,0:T(8,128)} %param.8) | copy-start | bytes 589828
  29.6 23.3 %collective-permute-start.5 = (f32[384,1024]{1,0:T(8,128)S(1)}, f32[384,1024]{1,0:T(8,128)S(1)}, u32[]{:S(2)}, u32[]{:S(2)}) collective-permute-start(f32[384,1024]{1,0:T(8,128)S(1)} %get-tuple-element.33), channel_id=1, source_target_pairs={{0,4},{4,0},{8,12},{12,8},{16,20},{20,16},{24,28},{28,24},{32,36},... | collective-permute-start | bytes 4718600 | tf_op jit(solution)/shard_map/ppermute | solution.py:390
  31.6 21.4 %collective-permute-start.6 = (f32[288,1024]{1,0:T(8,128)S(1)}, f32[288,1024]{1,0:T(8,128)S(1)}, u32[]{:S(2)}, u32[]{:S(2)}) collective-permute-start(f32[288,1024]{1,0:T(8,128)S(1)} %get-tuple-element.25.first_ref), channel_id=1, source_target_pairs={{12,4},{0,8},{20,12},{8,16},{28,20},{16,24},{36,28},{24,32},{44,36... | collective-permute-start | bytes 3538952 | tf_op jit(solution)/shard_map/ppermute | solution.py:366
  33.5 23.7 %collective-permute-start.7 = (f32[96,1024]{1,0:T(8,128)S(1)}, f32[96,1024]{1,0:T(8,128)S(1)}, u32[]{:S(2)}, u32[]{:S(2)}) collective-permute-start(f32[96,1024]{1,0:T(8,128)S(1)} %get-tuple-element.26.last_ref), channel_id=1, source_target_pairs={{12,4},{0,8},{20,12},{8,16},{28,20},{16,24},{36,28},{24,32},{44,36... | collective-permute-start | bytes 1179656 | tf_op jit(solution)/shard_map/ppermute | solution.py:367

commit v4 on v3

--- a/solution.py
+++ b/solution.py
@@ -13,7 +13,7 @@
 HZ = 24
 LANES = 128
 TILE = 256
-EDGE = 32
+EDGE = HZ
 LAST_STEPS = 2
 VMEM_BYTES = 16 * 2**20
 
@@ -43,28 +43,31 @@
     return jnp.dot(a, b, preferred_element_type=f32)
 
 
-def spread(packed, last):
+def spread(packed, last, count):
     pieces = []
     for group in range(LANES // EDGE):
         shift = (LANES - EDGE if last else 0) - group * EDGE
         pieces.append(pltpu.roll(packed, shift % LANES, 1) if shift else packed)
-    return jnp.concatenate(pieces, axis=0)
-
-
-def gathered(edge, last):
-    count = edge.shape[0] // (LANES // EDGE)
-    lane = lax.broadcasted_iota(jnp.int32, (count, LANES), 1) // EDGE
+    return jnp.concatenate(pieces, axis=0)[:count]
+
+
+def gathered(edge, last, count):
+    lane = lax.broadcasted_iota(jnp.int32, (count, LANES), 1)
     total = jnp.zeros((count, LANES), f32)
     for group in range(LANES // EDGE):
         piece = edge[group * count : (group + 1) * count]
+        if piece.shape[0] < count:
+            fill = jnp.zeros((count - piece.shape[0], LANES), f32)
+            piece = jnp.concatenate([piece, fill], axis=0)
         shift = group * EDGE - (LANES - EDGE if last else 0)
-        total = jnp.where(lane == group, pltpu.roll(piece, shift % LANES, 1) if shift else piece, total)
+        here = (lane >= group * EDGE) & (lane < (group + 1) * EDGE)
+        total = jnp.where(here, pltpu.roll(piece, shift % LANES, 1) if shift else piece, total)
     return total
 
 
 def pack_kernel(first_ref, last_ref, right_ref, left_ref):
-    right_ref[...] = gathered(first_ref[...], False)
-    left_ref[...] = gathered(last_ref[...], True)
+    right_ref[...] = gathered(first_ref[...], False, right_ref.shape[0])
+    left_ref[...] = gathered(last_ref[...], True, left_ref.shape[0])
 
 
 def put(high_ref, low_ref, start, value):
@@ -79,10 +82,10 @@
 
 def fill_outer(x_ref, left, right, high_ref, low_ref):
     own = TILE + LANES
-    put(high_ref, low_ref, 0, spread(left, True))
+    put(high_ref, low_ref, 0, spread(left, True, x_ref.shape[0]))
     put(high_ref, low_ref, LANES, x_ref[:, :own])
     put(high_ref, low_ref, LANES + own, x_ref[:, x_ref.shape[1] - own :])
-    put(high_ref, low_ref, LANES + 2 * own, spread(right, False))
+    put(high_ref, low_ref, LANES + 2 * own, spread(right, False, x_ref.shape[0]))
 
 
 def filtered(high_ref, low_ref, band_ref, start):
@@ -156,9 +159,9 @@
 ):
     count = edge_ref.shape[0] // 2
     width = far_ref.shape[1]
-    put(high_ref, low_ref, 0, spread(edge_ref[:count, :], True))
+    put(high_ref, low_ref, 0, spread(edge_ref[:count, :], True, far_ref.shape[0]))
     put(high_ref, low_ref, LANES, far_ref[...])
-    put(high_ref, low_ref, LANES + width, spread(edge_ref[count:, :], False))
+    put(high_ref, low_ref, LANES + width, spread(edge_ref[count:, :], False, far_ref.shape[0]))
     for at in range(0, width, TILE):
         put(far_high_ref, far_low_ref, at, filtered(high_ref, low_ref, band_ref, at))
 
@@ -172,7 +175,7 @@
 
 def some_steps(
     base, mine_ref, theirs_ref, near_ref, weight_ref, row_ref, before_ref, velocity_ref,
-    made_ref, field_ref, sems,
+    state_ref, made_ref, field_ref, sems,
 ):
     rows = weight_ref.shape[0]
     repeat = near_ref.shape[1] // LANES
@@ -181,10 +184,22 @@
         return jnp.concatenate([row_ref[index]] * repeat, axis=1)
 
     copies = []
-    for step in range(near_ref.shape[0] // (3 * rows)):
+
+    def send(source, target):
+        copy = pltpu.make_async_copy(source, target, sems.at[len(copies)])
+        copy.start()
+        copies.append(copy)
+
+    def made(at, value):
+        made_ref[pl.ds(at, rows), :] = value
+        send(made_ref.at[pl.ds(at, rows)], velocity_ref.at[pl.ds(base + at, rows)])
+
+    steps = near_ref.shape[0] // (3 * rows)
+    for step in range(steps):
         field = []
+        start = step * 3 * rows
         for part in range(3):
-            at = (step * 3 + part) * rows
+            at = start + part * rows
             of = pl.ds(part * rows, rows)
             high, low = halves(near_ref[pl.ds(at, rows), :])
             total = mine_ref[pl.ds(base + at, rows), :] + theirs_ref[pl.ds(base + at, rows), :]
@@ -193,44 +208,36 @@
             now = row(part) * before + row(3 + part) * total
             field_ref[of, :] = now
             field.append(now)
-        at = step * 3 * rows
-        made_ref[pl.ds(at, rows), :] = row(12) + row(6) * field[0]
-        made_ref[pl.ds(at + rows, rows), :] = row(7) * field[0] + row(8) * field[1]
-        made_ref[pl.ds(at + 2 * rows, rows), :] = (
-            row(9) * field[0] + row(10) * field[1] + row(11) * field[2]
-        )
-        copy = pltpu.make_async_copy(
-            made_ref.at[pl.ds(at, 3 * rows)], velocity_ref.at[pl.ds(base + at, 3 * rows)],
-            sems.at[step],
-        )
-        copy.start()
-        copies.append(copy)
-    return copies
+            if state_ref is not None and step == steps - 1:
+                send(field_ref.at[of], state_ref.at[of])
+            if part == 0:
+                made(at, row(12) + row(6) * field[0])
+            elif part == 1:
+                made(at, row(7) * field[0] + row(8) * field[1])
+            else:
+                made(at, row(9) * field[0] + row(10) * field[1] + row(11) * field[2])
+    for copy in copies:
+        copy.wait()
 
 
 def first_steps_kernel(
     mine_ref, theirs_ref, near_ref, weight_ref, row_ref, before_ref, velocity_ref, field_ref,
     made_ref, sems,
 ):
-    for copy in some_steps(
+    some_steps(
         0, mine_ref, theirs_ref, near_ref, weight_ref, row_ref, before_ref, velocity_ref,
-        made_ref, field_ref, sems,
-    ):
-        copy.wait()
+        None, made_ref, field_ref, sems,
+    )
 
 
 def last_steps_kernel(
     _, mine_ref, theirs_ref, near_ref, weight_ref, row_ref, before_ref, velocity_ref, state_ref,
     made_ref, field_ref, sems,
 ):
-    copies = some_steps(
+    some_steps(
         mine_ref.shape[0] - near_ref.shape[0], mine_ref, theirs_ref, near_ref, weight_ref,
-        row_ref, before_ref, velocity_ref, made_ref, field_ref, sems,
-    )
-    copy = pltpu.make_async_copy(field_ref, state_ref, sems.at[len(copies)])
-    copy.start()
-    for one in copies + [copy]:
-        one.wait()
+        row_ref, before_ref, velocity_ref, state_ref, made_ref, field_ref, sems,
+    )
 
 
 WHOLE = pl.BlockSpec(memory_space=pltpu.VMEM)
@@ -326,7 +333,7 @@
 
     x = random_planes.reshape(steps * parts * rows, width)
     count = x.shape[0]
-    packed_rows = count * EDGE // LANES
+    packed_rows = -(-count // (8 * (LANES // EDGE))) * 8
     far = lax.ppermute(x, "wall", far_pairs)
     packed = pltpu.VMEM((packed_rows, LANES), f32)
     mine_right, mine_left = call(
@@ -394,7 +401,7 @@
     velocity, field = call(
         first_steps_kernel,
         (jax.ShapeDtypeStruct(x.shape, f32), pltpu.VMEM(line, f32)),
-        [pltpu.VMEM((split, width), f32), pltpu.SemaphoreType.DMA((steps,))],
+        [pltpu.VMEM((split, width), f32), pltpu.SemaphoreType.DMA((3 * steps,))],
         wall_flops, mine, theirs, vmem(near_first), near_w, per_row,
         vmem(previous.reshape(line)), out_specs=(anywhere, WHOLE),
     )
@@ -403,7 +410,7 @@
         (jax.ShapeDtypeStruct(x.shape, f32), jax.ShapeDtypeStruct(line, f32)),
         [
             pltpu.VMEM((count - split, width), f32), pltpu.VMEM(line, f32),
-            pltpu.SemaphoreType.DMA((steps + 1,)),
+            pltpu.SemaphoreType.DMA((3 * steps + 3,)),
         ],
         wall_flops, velocity, mine, theirs, vmem(near_last), near_w, per_row, vmem(field),
         in_specs=[anywhere] + [WHOLE] * 6, out_specs=(anywhere, anywhere),

time: 58.6 us -> 58.6 us (level)
  no operation moved by 1% of the time
where the time goes in v4:
time: 58.6 us; the launch traced here: 58.2 us
  waiting for transfers between devices  25.3 us (43%)
  starting transfers between devices  21.1 us (36%)
  Pallas kernels  11 us (19%)
  between operations  0.81 us (1%)
    ppermute x1, waiting for transfers between devices, planes(): near_first = lax.ppermute(own_first, 'wall', near_pairs)  17.6 us
    pallas_call x8, Pallas kernels, call(): pl.pallas_call(kernel, out_shape=out, in_specs=in_specs or [WHOLE] * len(...  11 us
    ppermute x1, starting transfers between devices, planes(): far = lax.ppermute(x, 'wall', far_pairs)  4.04 us
    ppermute x1, starting transfers between devices, planes(): far_edges = lax.ppermute(far_edges, 'wall', far_pairs)  3.54 us
    ppermute x1, starting transfers between devices, planes(): right = lax.ppermute(mine_right, 'span', backward)  3.46 us
    ppermute x1, waiting for transfers between devices, planes(): near_last = lax.ppermute(own_last, 'wall', near_pairs)  2.7 us
    ppermute x1, starting transfers between devices, planes(): left = lax.ppermute(mine_left, 'span', forward)  2.39 us
    ppermute x1, waiting for transfers between devices, planes(): far_edges = lax.ppermute(far_edges, 'wall', far_pairs)  2.17 us
  transfers between devices with their start and end apart: 8, of which 5 were waited for; matrix products, arithmetic and copies ran while one was open for 0% of the time, Pallas kernels for 12%

profile of v4, /device:TPU:262, one launch (start us, length us, event | category | flops | bytes accessed | tf_op | source)
XLA Modules:
  0.0 58.2 jit_solution(13559884487725619974)
XLA Ops:
  0.6 0.0 copy-start
  0.6 4.0 %collective-permute-start.3 = (f32[384,1024]{1,0:T(8,128)}, f32[384,1024]{1,0:T(8,128)S(1)}, u32[]{:S(2)}, u32[]{:S(2)}) collective-permute-start(f32[384,1024]{1,0:T(8,128)} %bitcast.4), channel_id=1, source_target_pairs={{8,4},{4,8},{16,12},{12,16},{24,20},{20,24},{32,28},{28,32},{40,36... | collective-permute-start | bytes 4718600 | tf_op jit(solution)/shard_map/ppermute | solution.py:337
  4.7 1.2 %shard_map.87 = (f32[80,128]{1,0:T(8,128)S(1)}, f32[80,128]{1,0:T(8,128)S(1)}) custom-call(f32[384,1024]{1,0:T(8,128)} %bitcast.5, f32[384,1024]{1,0:T(8,128)} %bitcast.6), custom_call_target="tpu_custom_call" | custom-call | bytes 3145728 | tf_op jit(solution)/shard_map/pallas_call | solution.py:256
  5.9 2.4 %collective-permute-start = (f32[80,128]{1,0:T(8,128)S(1)}, f32[80,128]{1,0:T(8,128)S(1)}, u32[]{:S(2)}, u32[]{:S(2)}) collective-permute-start(f32[80,128]{1,0:T(8,128)S(1)} %get-tuple-element.22), channel_id=1, source_target_pairs={{0,1},{1,2},{2,3},{3,0},{4,5},{5,6},{6,7},{7,4},{8,9},{9,10},{10,1... | collective-permute-start | bytes 122888 | tf_op jit(solution)/shard_map/ppermute | solution.py:347
  8.3 3.5 %collective-permute-start.1 = (f32[80,128]{1,0:T(8,128)S(1)}, f32[80,128]{1,0:T(8,128)S(1)}, u32[]{:S(2)}, u32[]{:S(2)}) collective-permute-start(f32[80,128]{1,0:T(8,128)S(1)} %get-tuple-element.23), channel_id=1, source_target_pairs={{1,0},{2,1},{3,2},{0,3},{5,4},{6,5},{7,6},{4,7},{9,8},{10,9},{11,1... | collective-permute-start | bytes 122888 | tf_op jit(solution)/shard_map/ppermute | solution.py:348
  11.7 0.0 copy-done
  11.7 1.8 %shard_map.86 = (f32[384,512]{1,0:T(8,128)S(1)}, bf16[2,512,256]{2,1,0:T(8,128)(2,1)S(1)}) custom-call(f32[384,1024]{1,0:T(8,128)S(1)} %bitcast.7, bf16[2,512,256]{2,1,0:T(8,128)(2,1)} %constant.2.clone.band_hbm), custom_call_target="tpu_custom_call" | custom-call | flops 603979776 | bytes 2097152 | tf_op jit(solution)/shard_map/pallas_call | solution.py:256
  13.6 0.0 copy-start.4
  13.6 0.0 copy-start.2
  13.6 0.0 copy-start.3
  13.6 0.0 copy-start.5
  13.6 0.0 collective-permute-done.left_ref
  13.6 1.7 %collective-permute-done.1.right_ref = f32[80,128]{1,0:T(8,128)S(1)} collective-permute-done((f32[80,128]{1,0:T(8,128)S(1)}, f32[80,128]{1,0:T(8,128)S(1)}, u32[]{:S(2)}, u32[]{:S(2)}) %collective-permute-start.1) | collective-permute-done | bytes 40992 | tf_op jit(solution)/shard_map/ppermute | solution.py:348
  15.4 1.0 %shard_map.88 = (f32[288,1024]{1,0:T(8,128)S(1)}, f32[96,1024]{1,0:T(8,128)S(1)}, f32[160,128]{1,0:T(8,128)S(1)}) custom-call(f32[384,512]{1,0:T(8,128)S(1)} %get-tuple-element.21.inner_ref, f32[384,1024]{1,0:T(8,128)S(1)} %bitcast.8, f32[80,128]{1,0:T(8,128)S(1)} %collective-permute-done.left_ref, f32[80,128]{1,0:T(8,128)S(1)} %collective-permute-done.1.right_ref, ...), custom_call_target="tpu_custom_call" | custom-call | flops 603979776 | bytes 2965504 | tf_op jit(solution)/shard_map/pallas_call | solution.py:256
  16.3 3.5 %collective-permute-start.4 = (f32[160,128]{1,0:T(8,128)S(1)}, f32[160,128]{1,0:T(8,128)S(1)}, u32[]{:S(2)}, u32[]{:S(2)}) collective-permute-start(f32[160,128]{1,0:T(8,128)S(1)} %get-tuple-element.30), channel_id=1, source_target_pairs={{8,4},{4,8},{16,12},{12,16},{24,20},{20,24},{32,28},{28,32},{40,36... | collective-permute-start | bytes 245768 | tf_op jit(solution)/shard_map/ppermute | solution.py:375
  19.9 0.0 copy-done.4
  19.9 1.9 %collective-permute-start.2 = (s32[16]{0:T(128)S(1)}, s32[16]{0:T(128)S(1)}, u32[]{:S(2)}, u32[]{:S(2)}) collective-permute-start(s32[16]{0:T(128)S(1)} %copy-done.4), channel_id=1, source_target_pairs={{0,4},{4,0},{8,12},{12,8},{16,20},{20,16},{24,28},{28,24},{32,36},... | collective-permute-start | bytes 200 | tf_op jit(solution)/shard_map/ppermute | solution.py:376
  21.8 1.1 %collective-permute-done.2.other_ref = s32[16]{0:T(128)S(1)} collective-permute-done((s32[16]{0:T(128)S(1)}, s32[16]{0:T(128)S(1)}, u32[]{:S(2)}, u32[]{:S(2)}) %collective-permute-start.2) | collective-permute-done | bytes 96 | tf_op jit(solution)/shard_map/ppermute | solution.py:376
  22.9 0.0 copy-done.2
  22.9 0.0 copy-done.3
  22.9 0.0 copy-done.5
  23.0 0.8 %shard_map.89 = (bf16[32,48]{1,0:T(8,128)(2,1)S(1)}, bf16[32,48]{1,0:T(8,128)(2,1)S(1)}, bf16[16,48]{1,0:T(8,128)(2,1)S(1)}, f32[13,16,128]{2,1,0:T(8,128)S(1)}) custom-call(s32[16]{0:T(128)S(1)} %copy-done.4, s32[16]{0:T(128)S(1)} %collective-permute-done.2.other_ref, f32[3,16]{1,0:T(4,128)S(1)} %copy-done.3, f32[6,16]{1,0:T(8,128)S(1)} %copy-done.2, ...), custom_call_target="tpu_custom_call" | custom-call | bytes 768 | tf_op jit(solution)/shard_map/pallas_call | solution.py:256
  23.7 1.0 %shard_map.90 = (f32[384,1024]{1,0:T(8,128)S(1)}, f32[384,1024]{1,0:T(8,128)S(1)}) custom-call(f32[288,1024]{1,0:T(8,128)S(1)} %get-tuple-element.25.first_ref, f32[96,1024]{1,0:T(8,128)S(1)} %get-tuple-element.26.last_ref, bf16[32,48]{1,0:T(8,128)(2,1)S(1)} %get-tuple-element.27.weight_ref), custom_call_target="tpu_custom_call" | custom-call | flops 75497472 | bytes 1575936 | tf_op jit(solution)/shard_map/pallas_call | solution.py:256
  24.7 2.2 %collective-permute-done.4.edge_ref = f32[160,128]{1,0:T(8,128)S(1)} collective-permute-done((f32[160,128]{1,0:T(8,128)S(1)}, f32[160,128]{1,0:T(8,128)S(1)}, u32[]{:S(2)}, u32[]{:S(2)}) %collective-permute-start.4) | collective-permute-done | bytes 81952 | tf_op jit(solution)/shard_map/ppermute | solution.py:375
  26.9 0.0 collective-permute-done.3.far_ref
  26.9 0.0 copy-start.1
  26.9 2.5 %shard_map.91 = (f32[384,1024]{1,0:T(8,128)S(1)}, f32[384,1024]{1,0:T(8,128)S(1)}) custom-call(f32[384,1024]{1,0:T(8,128)S(1)} %get-tuple-element.28.mine_own_ref, f32[384,1024]{1,0:T(8,128)S(1)} %get-tuple-element.29.theirs_own_ref, f32[384,1024]{1,0:T(8,128)S(1)} %collective-permute-done.3.far_ref, f32[160,128]{1,0:T(8,128)S(1)} %collective-permute-done.4.edge_ref, ...), custom_call_target="tpu_custom_call" | custom-call | flops 1283457024 | bytes 5327872 | tf_op jit(solution)/shard_map/pallas_call | solution.py:256
  29.5 1.9 %collective-permute-start.5 = (f32[384,1024]{1,0:T(8,128)S(1)}, f32[384,1024]{1,0:T(8,128)S(1)}, u32[]{:S(2)}, u32[]{:S(2)}) collective-permute-start(f32[384,1024]{1,0:T(8,128)S(1)} %get-tuple-element.33), channel_id=1, source_target_pairs={{0,4},{4,0},{8,12},{12,8},{16,20},{20,16},{24,28},{28,24},{32,36},... | collective-permute-start | bytes 4718600 | tf_op jit(solution)/shard_map/ppermute | solution.py:397
  31.4 1.9 %collective-permute-start.6 = (f32[288,1024]{1,0:T(8,128)S(1)}, f32[288,1024]{1,0:T(8,128)S(1)}, u32[]{:S(2)}, u32[]{:S(2)}) collective-permute-start(f32[288,1024]{1,0:T(8,128)S(1)} %get-tuple-element.25.first_ref), channel_id=1, source_target_pairs={{12,4},{0,8},{20,12},{8,16},{28,20},{16,24},{36,28},{24,32},{44,36... | collective-permute-start | bytes 3538952 | tf_op jit(solution)/shard_map/ppermute | solution.py:373
  33.3 1.9 %collective-permute-start.7 = (f32[96,1024]{1,0:T(8,128)S(1)}, f32[96,1024]{1,0:T(8,128)S(1)}, u32[]{:S(2)}, u32[]{:S(2)}) collective-permute-start(f32[96,1024]{1,0:T(8,128)S(1)} %get-tuple-element.26.last_ref), channel_id=1, source_target_pairs={{12,4},{0,8},{20,12},{8,16},{28,20},{16,24},{36,28},{24,32},{44,36... | collective-permute-start | bytes 1179656 | tf_op jit(solution)/shard_map/ppermute | solution.py:374
  35.2 17.6 %collective-permute-done.6.near_ref = f32[288,1024]{1,0:T(8,128)S(1)} collective-permute-done((f32[288,1024]{1,0:T(8,128)S(1)}, f32[288,1024]{1,0:T(8,128)S(1)}, u32[]{:S(2)}, u32[]{:S(2)}) %collective-permute-start.6) | collective-permute-done | bytes 1179680 | tf_op jit(solution)/shard_map/ppermute | solution.py:373
  52.8 0.0 collective-permute-done.5.theirs_ref
  52.8 0.0 copy-done.1
  52.8 1.5 %shard_map.92 = (f32[384,1024]{1,0:T(8,128)}, f32[48,1024]{1,0:T(8,128)S(1)}) custom-call(f32[384,1024]{1,0:T(8,128)S(1)} %get-tuple-element.32.mine_ref, f32[384,1024]{1,0:T(8,128)S(1)} %collective-permute-done.5.theirs_ref, f32[288,1024]{1,0:T(8,128)S(1)} %collective-permute-done.6.near_ref, bf16[16,48]{1,0:T(8,128)(2,1)S(1)} %get-tuple-element.34.weight_ref, ...), custom_call_target="tpu_custom_call" | custom-call | flops 75497472 | bytes 4630016 | tf_op jit(solution)/shard_map/pallas_call | solution.py:256
  54.3 2.7 %collective-permute-done.7.near_ref = f32[96,1024]{1,0:T(8,128)S(1)} collective-permute-done((f32[96,1024]{1,0:T(8,128)S(1)}, f32[96,1024]{1,0:T(8,128)S(1)}, u32[]{:S(2)}, u32[]{:S(2)}) %collective-permute-start.7) | collective-permute-done | bytes 393248 | tf_op jit(solution)/shard_map/ppermute | solution.py:374
  57.0 1.2 %shard_map.93 = (f32[384,1024]{1,0:T(8,128)}, f32[48,1024]{1,0:T(8,128)}) custom-call(f32[384,1024]{1,0:T(8,128)} %get-tuple-element.36._, f32[384,1024]{1,0:T(8,128)S(1)} %get-tuple-element.32.mine_ref, f32[384,1024]{1,0:T(8,128)S(1)} %collective-permute-done.5.theirs_ref, ...), custom_call_target="tpu_custom_call", output_to_operand_aliasing={{0}: (0, {})} | custom-call | flops 75497472 | bytes 5416448 | tf_op jit(solution)/shard_map/pallas_call | solution.py:256
Async XLA Ops:
  0.6 11.1 %copy-start = (f32[8,3,16,1024]{3,2,1,0:T(8,128)S(1)}, f32[8,3,16,1024]{3,2,1,0:T(8,128)}, u32[]{:S(2)}) copy-start(f32[8,3,16,1024]{3,2,1,0:T(8,128)} %param.7) | copy-start | bytes 4718596
  0.6 26.3 %collective-permute-start.3 = (f32[384,1024]{1,0:T(8,128)}, f32[384,1024]{1,0:T(8,128)S(1)}, u32[]{:S(2)}, u32[]{:S(2)}) collective-permute-start(f32[384,1024]{1,0:T(8,128)} %bitcast.4), channel_id=1, source_target_pairs={{8,4},{4,8},{16,12},{12,16},{24,20},{20,24},{32,28},{28,32},{40,36... | collective-permute-start | bytes 4718600 | tf_op jit(solution)/shard_map/ppermute | solution.py:337
  5.9 7.8 %collective-permute-start = (f32[80,128]{1,0:T(8,128)S(1)}, f32[80,128]{1,0:T(8,128)S(1)}, u32[]{:S(2)}, u32[]{:S(2)}) collective-permute-start(f32[80,128]{1,0:T(8,128)S(1)} %get-tuple-element.22), channel_id=1, source_target_pairs={{0,1},{1,2},{2,3},{3,0},{4,5},{5,6},{6,7},{7,4},{8,9},{9,10},{10,1... | collective-permute-start | bytes 122888 | tf_op jit(solution)/shard_map/ppermute | solution.py:347
  8.3 7.1 %collective-permute-start.1 = (f32[80,128]{1,0:T(8,128)S(1)}, f32[80,128]{1,0:T(8,128)S(1)}, u32[]{:S(2)}, u32[]{:S(2)}) collective-permute-start(f32[80,128]{1,0:T(8,128)S(1)} %get-tuple-element.23), channel_id=1, source_target_pairs={{1,0},{2,1},{3,2},{0,3},{5,4},{6,5},{7,6},{4,7},{9,8},{10,9},{11,1... | collective-permute-start | bytes 122888 | tf_op jit(solution)/shard_map/ppermute | solution.py:348
  13.6 6.3 %copy-start.4 = (s32[16]{0:T(128)S(1)}, s32[16]{0:T(128)}, u32[]{:S(2)}) copy-start(s32[16]{0:T(128)} %width_ref.1) | copy-start | bytes 196
  13.6 9.3 %copy-start.2 = (f32[6,16]{1,0:T(8,128)S(1)}, f32[6,16]{1,0:T(8,128)}, u32[]{:S(2)}) copy-start(f32[6,16]{1,0:T(8,128)} %factor_ref.1) | copy-start | bytes 1156
  13.6 9.3 %copy-start.3 = (f32[3,16]{1,0:T(4,128)S(1)}, f32[3,16]{1,0:T(4,128)}, u32[]{:S(2)}) copy-start(f32[3,16]{1,0:T(4,128)} %scale_ref.1) | copy-start | bytes 580
  13.6 9.3 %copy-start.5 = (f32[16]{0:T(128)S(1)}, f32[16]{0:T(128)}, u32[]{:S(2)}) copy-start(f32[16]{0:T(128)} %mean_ref.1) | copy-start | bytes 196
  16.3 10.6 %collective-permute-start.4 = (f32[160,128]{1,0:T(8,128)S(1)}, f32[160,128]{1,0:T(8,128)S(1)}, u32[]{:S(2)}, u32[]{:S(2)}) collective-permute-start(f32[160,128]{1,0:T(8,128)S(1)} %get-tuple-element.30), channel_id=1, source_target_pairs={{8,4},{4,8},{16,12},{12,16},{24,20},{20,24},{32,28},{28,32},{40,36... | collective-permute-start | bytes 245768 | tf_op jit(solution)/shard_map/ppermute | solution.py:375
  19.9 3.1 %collective-permute-start.2 = (s32[16]{0:T(128)S(1)}, s32[16]{0:T(128)S(1)}, u32[]{:S(2)}, u32[]{:S(2)}) collective-permute-start(s32[16]{0:T(128)S(1)} %copy-done.4), channel_id=1, source_target_pairs={{0,4},{4,0},{8,12},{12,8},{16,20},{20,16},{24,28},{28,24},{32,36},... | collective-permute-start | bytes 200 | tf_op jit(solution)/shard_map/ppermute | solution.py:376
  26.9 25.9 %copy-start.1 = (f32[3,16,1024]{2,1,0:T(8,128)S(1)}, f32[3,16,1024]{2,1,0:T(8,128)}, u32[]{:S(2)}) copy-start(f32[3,16,1024]{2,1,0:T(8,128)} %param.8) | copy-start | bytes 589828
  29.5 23.3 %collective-permute-start.5 = (f32[384,1024]{1,0:T(8,128)S(1)}, f32[384,1024]{1,0:T(8,128)S(1)}, u32[]{:S(2)}, u32[]{:S(2)}) collective-permute-start(f32[384,1024]{1,0:T(8,128)S(1)} %get-tuple-element.33), channel_id=1, source_target_pairs={{0,4},{4,0},{8,12},{12,8},{16,20},{20,16},{24,28},{28,24},{32,36},... | collective-permute-start | bytes 4718600 | tf_op jit(solution)/shard_map/ppermute | solution.py:397
  31.4 21.4 %collective-permute-start.6 = (f32[288,1024]{1,0:T(8,128)S(1)}, f32[288,1024]{1,0:T(8,128)S(1)}, u32[]{:S(2)}, u32[]{:S(2)}) collective-permute-start(f32[288,1024]{1,0:T(8,128)S(1)} %get-tuple-element.25.first_ref), channel_id=1, source_target_pairs={{12,4},{0,8},{20,12},{8,16},{28,20},{16,24},{36,28},{24,32},{44,36... | collective-permute-start | bytes 3538952 | tf_op jit(solution)/shard_map/ppermute | solution.py:373
  33.3 23.7 %collective-permute-start.7 = (f32[96,1024]{1,0:T(8,128)S(1)}, f32[96,1024]{1,0:T(8,128)S(1)}, u32[]{:S(2)}, u32[]{:S(2)}) collective-permute-start(f32[96,1024]{1,0:T(8,128)S(1)} %get-tuple-element.26.last_ref), channel_id=1, source_target_pairs={{12,4},{0,8},{20,12},{8,16},{28,20},{16,24},{36,28},{24,32},{44,36... | collective-permute-start | bytes 1179656 | tf_op jit(solution)/shard_map/ppermute | solution.py:374
